TPU v7x, 256 devices: a whole 4x4x8 slice. The times are simulated.
256 devices in a mesh: ea: 64 (over z, x, core), sa: 4 (over y).
Axes of the slice: x: 4, y: 4, z: 8, core: 2. Of those that a mesh axis runs over, the one named last changes fastest.
Arguments:
- expert_hidden: bfloat16 [256, 1792, 512], P('ea', 'sa'), may hold values from -6 to 6
- down_weight: bfloat16 [256, 512, 2048], P('ea'), may hold values from -0.25 to 0.25
- residual: bfloat16 [64, 512, 2048], P('ea', 'sa'), may hold values from -6 to 6
- expert_ids: int32 [64, 512, 10], P('ea', 'sa'), may hold values from 0 to 255, all different within a row; in each aligned block of 128 rows (0 to 127, 128 to 255, ..., all dimensions but the last counted through in order) at most 7 rows name the same one
- combine_weight: float32 [64, 512, 10], P('ea', 'sa'), may hold values from 0.05 to 0.3
- norm_gain: bfloat16 [2048], replicated, may hold values from 0.25 to 1.75
- value_weight: bfloat16 [2048, 2048], P('ea'), may hold values from -0.125 to 0.125
- queries: bfloat16 [64, 512, 1024], P('ea', 'sa'), may hold values from -6 to 6
- keys: bfloat16 [64, 512, 1024], P('ea', 'sa'), may hold values from -6 to 6
- log_decay: float32 [64, 512, 16], P('ea', 'sa'), may hold values from -1 to 0, as said below
- write_rate: float32 [64, 512, 16], P('ea', 'sa'), may hold values from 0.1 to 0.9
Outputs:
- head_out: bfloat16 [64, 512, 2048], P('ea', 'sa')
Inputs may be any that keep to these rules, and one draw needn't show every extreme that they name: `expert_ids`: each row names 10 different experts; among the rows of one device (aligned blocks of 128 rows) no expert is named more than 7 times, a bound that some block reaches. `log_decay`: below zero.
All inputs are finite; a program needn't handle non-finite values.
Results may differ from a plain program's by a relative error of at most 0.0066.
Values may be sent and summed in bfloat16 or wider, within the bound.
A program may use at most 128 MiB of HBM per device.

v0:
```python
import jax
import jax.numpy as jnp
from jax import lax
from jax.experimental import pallas as pl
from jax.experimental.pallas import tpu as pltpu
from jax.sharding import PartitionSpec as P

HV = 16
HK = 8
DK = 128
DV = 128
BF = jnp.bfloat16
F32 = jnp.float32


def mm(a, b, dims=((1,), (0,))):
    return lax.dot_general(a.astype(BF), b.astype(BF), (dims, ((), ())), preferred_element_type=F32)


def mm_full(a, b, dims=((1,), (0,))):
    return lax.dot_general(
        a, b, (dims, ((), ())), preferred_element_type=F32, precision=lax.Precision.HIGHEST
    )


def mm3(a, b):
    ah, bh = a.astype(BF), b.astype(BF)
    al = (a - ah.astype(F32)).astype(BF)
    bl = (b - bh.astype(F32)).astype(BF)
    return mm(ah, bh) + (mm(ah, bl) + mm(al, bh))


def unit_lower_inverses(lowers):
    n = lowers[0].shape[0]
    row = lax.broadcasted_iota(jnp.int32, (n, n), 0)
    col = lax.broadcasted_iota(jnp.int32, (n, n), 1)
    eye = (row == col).astype(F32)
    size = 16
    same = (row // size) == (col // size)
    powers = [jnp.where(same, -low, 0.0) for low in lowers]
    outs = [eye + p for p in powers]
    for _ in range(3):
        powers = [mm3(p, p) for p in powers]
        outs = [o + mm3(p, o) for p, o in zip(powers, outs)]
    while size < n:
        join = ((row // (2 * size)) == (col // (2 * size))) & ((row // size) > (col // size))
        parts = [mm3(jnp.where(join, low, 0.0), o) for low, o in zip(lowers, outs)]
        outs = [o - mm3(o, p) for o, p in zip(outs, parts)]
        size *= 2
    return outs


def prepare_kernel(q_ref, k_ref, sum_ref, rate_ref, sumt_ref, ratet_ref, mbo_ref, a_ref, g_ref, *, pairs):
    n = q_ref.shape[0]
    row = lax.broadcasted_iota(jnp.int32, (n, n), 0)
    col = lax.broadcasted_iota(jnp.int32, (n, n), 1)
    inclusive = row >= col
    strict = row > col
    eye = (row == col).astype(F32)
    ones = jnp.ones((8, DK), F32)
    base = pl.program_id(0) * (2 * pairs)
    lane = lax.broadcasted_iota(jnp.int32, (n, HV), 1)
    heads, lowers = [], []
    for pair in range(pairs):
        q = q_ref[:, pair * DK : (pair + 1) * DK]
        k = k_ref[:, pair * DK : (pair + 1) * DK]
        qf, kf = q.astype(F32), k.astype(F32)
        kn_col = lax.rsqrt(jnp.sum(kf * kf, axis=-1, keepdims=True) + 1e-06)
        qn_col = lax.rsqrt(jnp.sum(qf * qf, axis=-1, keepdims=True) + 1e-06) * DK ** (-0.5)
        kn_row = lax.rsqrt(mm_full(ones, kf * kf, ((1,), (1,)))[:1] + 1e-06)
        kk = mm(k, k, ((1,), (1,))) * kn_col * kn_row
        qk = mm(q, k, ((1,), (1,))) * qn_col * kn_row
        for half in range(2):
            h = 2 * pair + half
            pick = lane == base + h
            g_col = jnp.sum(jnp.where(pick, sum_ref[...], 0.0), axis=1, keepdims=True)
            rate_col = jnp.sum(jnp.where(pick, rate_ref[...], 0.0), axis=1, keepdims=True)
            g_row = sumt_ref[h : h + 1, :]
            rate_row = ratet_ref[h : h + 1, :]
            ratio = jnp.where(inclusive, jnp.exp(jnp.where(inclusive, g_col - g_row, 0.0)), 0.0)
            lowers.append(jnp.where(strict, rate_col * ratio * kk, 0.0))
            heads.append((h, q, k, qf, kf, kn_col, qn_col, kn_row, g_col, g_row, rate_row, qk * ratio))
    inverses = unit_lower_inverses(lowers)
    for inverse, (h, q, k, qf, kf, kn_col, qn_col, kn_row, g_col, g_row, rate_row, scores) in zip(inverses, heads):
        mix = inverse * rate_row
        emat = mm(mix * (jnp.exp(g_row) * kn_row), k)
        last = g_col[n - 1 : n, :]
        ktail = kf * (kn_col * jnp.exp(last - g_col))
        a_ref[h] = (jnp.exp(last) * eye - mm(ktail, emat, ((0,), (0,)))).astype(BF)
        mbo_ref[h, :n, :] = mm(scores, mix).astype(BF)
        mbo_ref[h, n:, :] = mm(ktail, mix, ((0,), (0,))).astype(BF)
        g_ref[h] = (jnp.exp(g_col) * qn_col * qf - mm(scores, emat)).astype(BF)


def prepare(queries, keys, summed, rate):
    n = queries.shape[0]
    pairs = 4
    steps = HK // pairs
    heads = 2 * pairs
    return pl.pallas_call(
        lambda *refs: prepare_kernel(*refs, pairs=pairs),
        grid=(steps,),
        in_specs=[
            pl.BlockSpec((n, pairs * DK), lambda i: (0, i)),
            pl.BlockSpec((n, pairs * DK), lambda i: (0, i)),
            pl.BlockSpec((n, HV), lambda i: (0, 0)),
            pl.BlockSpec((n, HV), lambda i: (0, 0)),
            pl.BlockSpec((heads, n), lambda i: (i, 0)),
            pl.BlockSpec((heads, n), lambda i: (i, 0)),
        ],
        out_specs=[
            pl.BlockSpec((heads, 2 * n, n), lambda i: (i, 0, 0)),
            pl.BlockSpec((heads, DK, DK), lambda i: (i, 0, 0)),
            pl.BlockSpec((heads, n, DK), lambda i: (i, 0, 0)),
        ],
        out_shape=[
            jax.ShapeDtypeStruct((HV, 2 * n, n), BF),
            jax.ShapeDtypeStruct((HV, DK, DK), BF),
            jax.ShapeDtypeStruct((HV, n, DK), BF),
        ],
        cost_estimate=pl.CostEstimate(flops=4_000_000_000, bytes_accessed=4_000_000, transcendentals=0),
        name="prepare",
    )(queries, keys, summed, rate, summed.T, rate.T)


def reach_kernel(g_ref, a1_ref, a2_ref, out_ref):
    for h in range(g_ref.shape[0]):
        g = g_ref[h]
        g2 = mm(g, a1_ref[h]).astype(BF)
        out_ref[h, :, :DK] = g
        out_ref[h, :, DK : 2 * DK] = g2
        out_ref[h, :, 2 * DK :] = mm(g2, a2_ref[h]).astype(BF)


def reach(gmat, a1, a2):
    heads, n, _ = gmat.shape
    return pl.pallas_call(
        reach_kernel,
        out_shape=jax.ShapeDtypeStruct((heads, n, 3 * DK), BF),
        cost_estimate=pl.CostEstimate(flops=200_000_000, bytes_accessed=4_000_000, transcendentals=0),
        name="reach",
    )(gmat, a1, a2)


def values_kernel(moe_ref, res_ref, gain_ref, w_ref, mbo_ref, zero_ref, b_ref, normed):
    n = res_ref.shape[0]

    @pl.when(pl.program_id(0) == 0)
    def _():
        stream = (res_ref[...].astype(F32) + moe_ref[...].astype(F32)).astype(BF).astype(F32)
        scale = lax.rsqrt(jnp.mean(stream * stream, axis=-1, keepdims=True) + 1e-06)
        normed[...] = (stream * scale * gain_ref[...].astype(F32)).astype(BF)

    values = mm(normed[...], w_ref[...]).astype(BF)
    for h in range(mbo_ref.shape[0]):
        both = mm(mbo_ref[h], values[:, h * DV : (h + 1) * DV])
        zero_ref[:, h * DV : (h + 1) * DV] = both[:n]
        b_ref[h] = both[n:].astype(BF)


def project(moe, residual, gain, weight, mbo):
    n, width = residual.shape
    heads = 4
    return pl.pallas_call(
        values_kernel,
        grid=(HV // heads,),
        in_specs=[
            pl.BlockSpec((n, width), lambda i: (0, 0)),
            pl.BlockSpec((n, width), lambda i: (0, 0)),
            pl.BlockSpec((1, width), lambda i: (0, 0)),
            pl.BlockSpec((width, heads * DV), lambda i: (0, i)),
            pl.BlockSpec((heads, 2 * n, n), lambda i: (i, 0, 0)),
        ],
        out_specs=[
            pl.BlockSpec((n, heads * DV), lambda i: (0, i)),
            pl.BlockSpec((heads, DK, DV), lambda i: (i, 0, 0)),
        ],
        out_shape=[
            jax.ShapeDtypeStruct((n, HV * DV), F32),
            jax.ShapeDtypeStruct((HV, DK, DV), BF),
        ],
        scratch_shapes=[pltpu.VMEM((n, width), BF)],
        cost_estimate=pl.CostEstimate(flops=1_200_000_000, bytes_accessed=12_000_000, transcendentals=0),
        name="project",
    )(moe, residual, gain.reshape(1, width), weight, mbo)


def finish_kernel(zero_ref, reach_ref, b1_ref, b2_ref, b3_ref, out_ref):
    for h in range(reach_ref.shape[0]):
        total = zero_ref[:, h * DV : (h + 1) * DV]
        for d, b_ref in enumerate((b1_ref, b2_ref, b3_ref)):
            total += mm(reach_ref[h, :, d * DK : (d + 1) * DK], b_ref[h])
        out_ref[:, h * DV : (h + 1) * DV] = total.astype(BF)


def finish(zero, reached, b1, b2, b3):
    n = zero.shape[0]
    return pl.pallas_call(
        finish_kernel,
        out_shape=jax.ShapeDtypeStruct((n, HV * DV), BF),
        name="finish",
    )(zero, reached, b1, b2, b3)


def on_device(
    shape_x,
    expert_hidden,
    down_weight,
    residual,
    expert_ids,
    combine_weight,
    norm_gain,
    value_weight,
    queries,
    keys,
    log_decay,
    write_rate,
):
    n_ea = lax.axis_size("ea")
    n_sa = lax.axis_size("sa")
    exp_dev, ff_units, width = down_weight.shape
    cap = expert_hidden.shape[1] // n_ea
    experts = exp_dev * n_ea
    tokens = residual.shape[1]
    top = expert_ids.shape[2]
    plane = shape_x
    layers = n_ea // plane
    in_plane = [[z * plane + i for i in range(plane)] for z in range(layers)]
    across = [[z * plane + i for z in range(layers)] for i in range(plane)]
    me = lax.axis_index("ea")
    my_layer = me // plane

    hidden = expert_hidden.reshape(exp_dev, layers, plane, cap, ff_units).transpose(2, 0, 1, 3, 4)
    hidden = hidden.reshape(plane, exp_dev, layers * cap, ff_units)
    produced = jnp.einsum("perf,efd->perd", hidden, down_weight, preferred_element_type=F32).astype(BF)
    received = lax.all_to_all(
        produced, "ea", split_axis=0, concat_axis=0, tiled=True, axis_index_groups=in_plane
    )
    per_layer = plane * exp_dev * layers * cap
    received = received.reshape(per_layer, width)

    ids = expert_ids[0]
    onehot = ids[:, :, None] == jnp.arange(experts, dtype=jnp.int32)[None, None, :]
    counts = jnp.sum(onehot.astype(F32), axis=1)
    earlier = lax.broadcasted_iota(jnp.int32, (tokens, tokens), 0) > lax.broadcasted_iota(
        jnp.int32, (tokens, tokens), 1
    )
    prior = mm(earlier, counts)
    slots = jnp.sum(jnp.where(onehot, prior[:, None, :], 0.0), axis=-1)
    place = (ids // exp_dev) * (exp_dev * layers * cap) + (ids % exp_dev) * (layers * cap)
    route = jnp.concatenate([place.astype(F32) + slots, combine_weight[0]], axis=1)
    routes = lax.all_gather(route, "ea", axis=0, axis_index_groups=across)
    offset = (jnp.arange(layers) * cap - my_layer * per_layer).astype(F32)[:, None, None]
    where_to = (routes[:, :, :top] + offset).reshape(layers * tokens, top).astype(jnp.int32)
    amount = routes[:, :, top:].reshape(layers * tokens, top)
    slot_of = lax.broadcasted_iota(jnp.int32, (layers * tokens, per_layer), 1)
    mixing = jnp.zeros((layers * tokens, per_layer), F32)
    for i in range(top):
        mixing = mixing + jnp.where(slot_of == where_to[:, i : i + 1], amount[:, i : i + 1], 0.0)
    partial = mm(mixing, received).astype(BF)
    moe = lax.psum_scatter(
        partial.reshape(layers, tokens, width),
        "ea",
        scatter_dimension=0,
        axis_index_groups=across,
        tiled=False,
    )

    summed = jnp.cumsum(log_decay[0], axis=0)
    mbo, amat, gmat = prepare(queries[0], keys[0], summed, write_rate[0])

    def shifted(field, by):
        return lax.ppermute(field, "sa", [(i, i + by) for i in range(n_sa - by)])

    reached = reach(gmat, shifted(amat, 1), shifted(amat, 2))
    full_weight = lax.all_gather(value_weight, "ea", axis=0, tiled=True)
    zero, bmat = project(moe, residual[0], norm_gain, full_weight, mbo)
    out = finish(zero, reached, shifted(bmat, 1), shifted(bmat, 2), shifted(bmat, 3))
    return out[None]


def solution(mesh):
    def body(*args):
        return on_device(8, *args)

    return jax.shard_map(
        body,
        mesh=mesh,
        in_specs=(
            P("ea", "sa", None),
            P("ea", None, None),
            P("ea", "sa", None),
            P("ea", "sa", None),
            P("ea", "sa", None),
            P(),
            P("ea", None),
            P("ea", "sa", None),
            P("ea", "sa", None),
            P("ea", "sa", None),
            P("ea", "sa", None),
        ),
        out_specs=P("ea", "sa", None),
        check_vma=False,
    )
```

profile of v0, /device:TPU:24, one launch (start us, length us, event | category | flops | bytes accessed | tf_op | source)
XLA Modules:
  0.0 289.0 jit_solution(9478699847965231364)
XLA Ops:
  7.4 2.9 %copy.33 = bf16[4,448,512]{2,0,1:T(4,128)(2,1)S(1)} copy(bf16[4,448,512]{2,1,0:T(8,128)(2,1)} %param.11) | data formatting | bytes 3670016 | tf_op args[0]
  10.3 0.4 copy.34
  10.7 9.5 %convert_bitcast_fusion = bf16[8,4,56,2048]{3,2,0,1:T(8,128)(2,1)} fusion(bf16[4,512,2048]{2,1,0:T(8,128)(2,1)} %param.12, bf16[8,4,56,512]{3,0,2,1:T(8,128)(2,1)S(1)} %bitcast.75), kind=kOutput, calls=%fused_computation.2 | convolution fusion | flops 3761766400 | bytes 17563648 | tf_op jit(solution)/shard_map/perf,efd->perd/dot_general | solution.py:235
  20.2 7.5 %copy.36 = bf16[8,4,56,2048]{3,2,1,0:T(8,128)(2,1)} copy(bf16[8,4,56,2048]{3,2,0,1:T(8,128)(2,1)} %convert_bitcast_fusion) | data formatting | bytes 14680064 | tf_op jit(solution)/shard_map/convert_element_type | solution.py:235
  27.7 0.0 copy-start.9
  27.7 0.0 copy-start.6
  27.7 5.0 %all-to-all-start = ((bf16[8,4,56,2048]{3,2,1,0:T(8,128)(2,1)}), bf16[8,4,56,2048]{3,2,1,0:T(8,128)(2,1)}, u32[]{:S(2)}, u32[]{:S(2)}) async-start(bf16[8,4,56,2048]{3,2,1,0:T(8,128)(2,1)} %copy.36), calls=%async_computation | async-start | bytes 14680064 | tf_op jit(solution)/shard_map/all_to_all | solution.py:236
  32.7 0.0 reduce-scatter.2.cloned.1.call-start
  32.7 0.0 copy-done.9
  32.7 0.0 copy-done.6
  32.8 0.2 convert_reduce_fusion
  33.0 0.1 fusion.26
  33.1 0.5 select_reduce_fusion
  33.7 28.4 %all-gather = f32[1024,20]{0,1:T(8,128)S(1)} all-gather(f32[128,20]{0,1:T(8,128)S(1)} %pad_maximum_fusion), channel_id=2, replica_groups={{0,32,64,96,128,160,192,224},{4,36,68,100,132,164,196,228},{8,40,72,104..., dimensions={0}, use_global_device_ids=true | all-gather | bytes 92160 | tf_op jit(solution)/shard_map/all_gather | solution.py:252
  62.1 0.1 fusion.29
  62.4 53.6 %all-to-all-done = bf16[8,4,56,2048]{3,2,1,0:T(8,128)(2,1)} async-done(((bf16[8,4,56,2048]{3,2,1,0:T(8,128)(2,1)}), bf16[8,4,56,2048]{3,2,1,0:T(8,128)(2,1)}, u32[]{:S(2)}, u32[]{:S(2)}) %all-to-all-start) | async-done | bytes 7340064 | tf_op jit(solution)/shard_map/all_to_all | solution.py:236
  116.0 0.0 copy-start.7
  116.0 0.0 copy-start.8
  116.0 20.4 %convolution_convert_fusion = bf16[1024,2048]{1,0:T(8,128)(2,1)} fusion(bf16[1792,2048]{1,0:T(8,128)(2,1)} %bitcast.26, f32[1024]{0:T(1024)S(1)} %bitcast.92, s32[1024]{0:T(1024)S(1)} %bitcast.102, f32[1024]{0:T(1024)S(1)} %bitcast.93, s32[1024]{0:T(1024)S(1)} %bitcast.103, f32[1024]{0:T(1024)S(1)} %bitcast.94, s32[1024]{0:T(1024)S(1)} %bitcast.104, ...), kind=kOutput, calls=%fused_computation.14 | convolution fusion | flops 7573340160 | bytes 11616256 | tf_op jit(solution)/shard_map/dot_general | solution.py:17
  136.5 0.0 reduce-scatter.2.cloned.1.call-update
  136.5 0.0 all-gather.3.cloned.1.call-start
  136.5 0.5 all-gather.3.cloned.1.call-update
  137.1 0.0 copy-done.7
  137.1 0.1 copy.37
  137.2 0.2 reduce_window_sum.11.refs_2_
  137.3 0.0 copy-start.5
  137.3 0.0 copy-done.8
  137.3 0.7 copy.39.refs_3_
  138.1 0.7 copy.38
  138.7 0.0 copy-done.5
  138.7 0.0 copy-start.10
  138.7 11.9 %prepare.1 = (bf16[16,256,128]{2,1,0:T(8,128)(2,1)}, bf16[16,128,128]{2,1,0:T(8,128)(2,1)}, bf16[16,128,128]{2,1,0:T(8,128)(2,1)}) custom-call(bf16[128,1024]{1,0:T(8,128)(2,1)} %bitcast.111, bf16[128,1024]{1,0:T(8,128)(2,1)} %bitcast.112, f32[128,16]{1,0:T(8,128)} %copy-done.5, f32[128,16]{1,0:T(8,128)} %copy.39.refs_3_, f32[16,128]{1,0:T(8,128)} %bitcast.90, ...), custom_call_target="tpu_custom_call" | custom-call | flops 4000000000 | bytes 4000000 | tf_op jit(solution)/shard_map/prepare/pallas_call | solution.py:100
  150.7 1.3 collective-permute-start
  152.0 1.3 collective-permute-start.1
  153.3 0.0 copy-done.10
  153.3 0.6 reshape.33.gain_ref
  153.9 43.5 %reduce-scatter.2.cloned.1.call-done = bf16[1,128,2048]{2,1,0:T(8,128)(2,1)} async-done(((bf16[8,128,2048]{2,1,0:T(8,128)(2,1)}), bf16[1,128,2048]{2,1,0:T(8,128)(2,1)}) %reduce-scatter.2.cloned.1.call-update) | async-done | bytes 524304 | tf_op jit(solution)/shard_map/reduce_scatter | solution.py:261
  197.4 42.6 %all-gather.3.cloned.1.call-done.w_ref = bf16[2048,2048]{1,0:T(8,128)(2,1)} async-done(((bf16[32,2048]{1,0:T(8,128)(2,1)}), bf16[2048,2048]{1,0:T(8,128)(2,1)}) %all-gather.3.cloned.1.call-update) | async-done | bytes 8388624 | tf_op jit(solution)/shard_map/all_gather | solution.py:276
  240.0 7.0 %project.1 = (f32[128,2048]{1,0:T(8,128)}, bf16[16,128,128]{2,1,0:T(8,128)(2,1)}) custom-call(bf16[128,2048]{1,0:T(8,128)(2,1)} %bitcast.77, bf16[128,2048]{1,0:T(8,128)(2,1)} %bitcast.76, bf16[1,2048]{1,0:T(2,128)(2,1)} %reshape.33.gain_ref, bf16[2048,2048]{1,0:T(8,128)(2,1)} %all-gather.3.cloned.1.call-done.w_ref, ...), custom_call_target="tpu_custom_call" | custom-call | flops 1200000000 | bytes 12000000 | tf_op jit(solution)/shard_map/project/pallas_call | solution.py:164
  247.1 1.3 collective-permute-start.2
  248.4 1.3 collective-permute-start.3
  249.7 1.3 collective-permute-start.4
  251.0 0.0 collective-permute-done.a1_ref
  251.0 0.0 copy-start.3
  251.0 0.0 collective-permute-done.1.a2_ref
  251.0 0.0 copy-start.4
  251.0 0.8 copy-done.3
  251.8 0.1 copy-done.4
  251.9 3.1 %reach.1.reach_ref = bf16[16,128,384]{2,1,0:T(8,128)(2,1)} custom-call(bf16[16,128,128]{2,1,0:T(8,128)(2,1)} %get-tuple-element.12.g_ref, bf16[16,128,128]{2,1,0:T(8,128)(2,1)} %copy-done.3, bf16[16,128,128]{2,1,0:T(8,128)(2,1)} %copy-done.4), custom_call_target="tpu_custom_call" | custom-call | flops 200000000 | bytes 4000000 | tf_op jit(solution)/shard_map/reach/pallas_call | solution.py:137
  255.0 8.3 %collective-permute-done.2.b1_ref = bf16[16,128,128]{2,1,0:T(8,128)(2,1)S(1)} collective-permute-done((bf16[16,128,128]{2,1,0:T(8,128)(2,1)}, bf16[16,128,128]{2,1,0:T(8,128)(2,1)S(1)}, u32[]{:S(2)}, u32[]{:S(2)}) %collective-permute-start.2) | collective-permute-done | bytes 524320 | tf_op jit(solution)/shard_map/ppermute | solution.py:273
  263.3 0.0 copy-start
  263.3 2.9 %collective-permute-done.3.b2_ref = bf16[16,128,128]{2,1,0:T(8,128)(2,1)S(1)} collective-permute-done((bf16[16,128,128]{2,1,0:T(8,128)(2,1)}, bf16[16,128,128]{2,1,0:T(8,128)(2,1)S(1)}, u32[]{:S(2)}, u32[]{:S(2)}) %collective-permute-start.3) | collective-permute-done | bytes 524320 | tf_op jit(solution)/shard_map/ppermute | solution.py:273
  266.2 0.0 copy-start.1
  266.2 11.1 %collective-permute-done.4.b3_ref = bf16[16,128,128]{2,1,0:T(8,128)(2,1)S(1)} collective-permute-done((bf16[16,128,128]{2,1,0:T(8,128)(2,1)}, bf16[16,128,128]{2,1,0:T(8,128)(2,1)S(1)}, u32[]{:S(2)}, u32[]{:S(2)}) %collective-permute-start.4) | collective-permute-done | bytes 524320 | tf_op jit(solution)/shard_map/ppermute | solution.py:273
  277.3 0.0 copy-start.2
  277.3 0.0 copy-done
  277.3 0.0 copy-done.1
  277.3 0.8 copy-done.2
  278.1 3.5 %finish.1 = bf16[128,2048]{1,0:T(8,128)(2,1)} custom-call(f32[128,2048]{1,0:T(8,128)} %get-tuple-element.11.zero_ref, bf16[16,128,384]{2,1,0:T(8,128)(2,1)} %reach.1.reach_ref, bf16[16,128,128]{2,1,0:T(8,128)(2,1)} %copy-done, bf16[16,128,128]{2,1,0:T(8,128)(2,1)} %copy-done.1, bf16[16,128,128]{2,1,0:T(8,128)(2,1)} %copy-done.2), custom_call_target="tpu_custom_call" | custom-call | tf_op jit(solution)/shard_map/finish/pallas_call | solution.py:198
  (13 shorter events, 0.2 us)
Async XLA Ops:
  27.7 5.0 %copy-start.9 = (f32[1,128,10]{1,0,2:T(1,128)S(1)}, f32[1,128,10]{1,0,2:T(1,128)}, u32[]{:S(2)}) copy-start(f32[1,128,10]{1,0,2:T(1,128)} %param.15) | copy-start | bytes 15364
  27.7 5.1 %copy-start.6 = (s32[1,128,10]{1,0,2:T(1,128)S(1)}, s32[1,128,10]{1,0,2:T(1,128)}, u32[]{:S(2)}) copy-start(s32[1,128,10]{1,0,2:T(1,128)} %param.14) | copy-start | bytes 15364
  27.7 88.3 %all-to-all-start = ((bf16[8,4,56,2048]{3,2,1,0:T(8,128)(2,1)}), bf16[8,4,56,2048]{3,2,1,0:T(8,128)(2,1)}, u32[]{:S(2)}, u32[]{:S(2)}) async-start(bf16[8,4,56,2048]{3,2,1,0:T(8,128)(2,1)} %copy.36), calls=%async_computation | async-start | bytes 14680064 | tf_op jit(solution)/shard_map/all_to_all | solution.py:236
  32.7 164.8 %reduce-scatter.2.cloned.1.call-start = ((), (), s32[]{:S(2)}) async-start(), calls=%async_computation.2 | async-start | bytes 4718592 | tf_op jit(solution)/shard_map/reduce_scatter | solution.py:261
  116.0 21.1 %copy-start.7 = (f32[1,128,16]{1,2,0:T(8,128)S(1)}, f32[1,128,16]{1,2,0:T(8,128)}, u32[]{:S(2)}) copy-start(f32[1,128,16]{1,2,0:T(8,128)} %param.20) | copy-start | bytes 24580
  116.0 21.3 %copy-start.8 = (f32[1,128,16]{1,2,0:T(8,128)S(1)}, f32[1,128,16]{1,2,0:T(8,128)}, u32[]{:S(2)}) copy-start(f32[1,128,16]{1,2,0:T(8,128)} %param.21) | copy-start | bytes 24580
  136.5 103.6 %all-gather.3.cloned.1.call-start = ((), (), s32[]{:S(2)}) async-start(), calls=%async_computation.3 | async-start | bytes 8519680 | tf_op jit(solution)/shard_map/all_gather | solution.py:276
  137.3 1.4 copy-start.5
  138.7 14.5 %copy-start.10 = (bf16[2048]{0:T(1024)(128)(2,1)S(1)}, bf16[2048]{0:T(1024)(128)(2,1)}, u32[]{:S(2)}) copy-start(bf16[2048]{0:T(1024)(128)(2,1)} %param.16) | copy-start | bytes 12292
  150.7 100.3 %collective-permute-start = (bf16[16,128,128]{2,1,0:T(8,128)(2,1)}, bf16[16,128,128]{2,1,0:T(8,128)(2,1)S(1)}, u32[]{:S(2)}, u32[]{:S(2)}) collective-permute-start(bf16[16,128,128]{2,1,0:T(8,128)(2,1)} %get-tuple-element.13), channel_id=1, source_target_pairs={{0,1},{1,2},{2,3},{4,5},{5,6},{6,7},{8,9},{9,10},{10,11},{12,13},{... | collective-permute-start | bytes 1572872 | tf_op jit(solution)/shard_map/ppermute | solution.py:273
  152.0 99.0 %collective-permute-start.1 = (bf16[16,128,128]{2,1,0:T(8,128)(2,1)}, bf16[16,128,128]{2,1,0:T(8,128)(2,1)S(1)}, u32[]{:S(2)}, u32[]{:S(2)}) collective-permute-start(bf16[16,128,128]{2,1,0:T(8,128)(2,1)} %get-tuple-element.13), channel_id=1, source_target_pairs={{0,2},{1,3},{4,6},{5,7},{8,10},{9,11},{12,14},{13,15},{16,18},{17,... | collective-permute-start | bytes 1572872 | tf_op jit(solution)/shard_map/ppermute | solution.py:273
  247.1 16.2 %collective-permute-start.2 = (bf16[16,128,128]{2,1,0:T(8,128)(2,1)}, bf16[16,128,128]{2,1,0:T(8,128)(2,1)S(1)}, u32[]{:S(2)}, u32[]{:S(2)}) collective-permute-start(bf16[16,128,128]{2,1,0:T(8,128)(2,1)} %get-tuple-element.14), channel_id=1, source_target_pairs={{0,1},{1,2},{2,3},{4,5},{5,6},{6,7},{8,9},{9,10},{10,11},{12,13},{... | collective-permute-start | bytes 1572872 | tf_op jit(solution)/shard_map/ppermute | solution.py:273
  248.4 17.8 %collective-permute-start.3 = (bf16[16,128,128]{2,1,0:T(8,128)(2,1)}, bf16[16,128,128]{2,1,0:T(8,128)(2,1)S(1)}, u32[]{:S(2)}, u32[]{:S(2)}) collective-permute-start(bf16[16,128,128]{2,1,0:T(8,128)(2,1)} %get-tuple-element.14), channel_id=1, source_target_pairs={{0,2},{1,3},{4,6},{5,7},{8,10},{9,11},{12,14},{13,15},{16,18},{17,... | collective-permute-start | bytes 1572872 | tf_op jit(solution)/shard_map/ppermute | solution.py:273
  249.7 27.6 %collective-permute-start.4 = (bf16[16,128,128]{2,1,0:T(8,128)(2,1)}, bf16[16,128,128]{2,1,0:T(8,128)(2,1)S(1)}, u32[]{:S(2)}, u32[]{:S(2)}) collective-permute-start(bf16[16,128,128]{2,1,0:T(8,128)(2,1)} %get-tuple-element.14), channel_id=1, source_target_pairs={{0,3},{4,7},{8,11},{12,15},{16,19},{20,23},{24,27},{28,31},{32,35}... | collective-permute-start | bytes 1572872 | tf_op jit(solution)/shard_map/ppermute | solution.py:273
  251.0 0.8 copy-start.3
  251.0 0.9 copy-start.4
  263.3 14.0 %copy-start = (bf16[16,128,128]{2,1,0:T(8,128)(2,1)}, bf16[16,128,128]{2,1,0:T(8,128)(2,1)S(1)}, u32[]{:S(2)}) copy-start(bf16[16,128,128]{2,1,0:T(8,128)(2,1)S(1)} %collective-permute-done.2.b1_ref) | copy-start | bytes 1572868
  266.2 11.1 %copy-start.1 = (bf16[16,128,128]{2,1,0:T(8,128)(2,1)}, bf16[16,128,128]{2,1,0:T(8,128)(2,1)S(1)}, u32[]{:S(2)}) copy-start(bf16[16,128,128]{2,1,0:T(8,128)(2,1)S(1)} %collective-permute-done.3.b2_ref) | copy-start | bytes 1572868
  277.3 0.8 copy-start.2
Sparse Core Ops, SparseCore 0:
  136.6 60.7 reduce-scatter.1
Sparse Core Ops, SparseCore 1:
  139.7 100.3 all-gather.2
where the time goes:
time: 290 us; the launch traced here: 289 us
  waiting for transfers between devices  163 us (56%)
  matrix products  30.1 us (10%)
  blocking collectives  28.4 us (10%)
  Pallas kernels  25.5 us (9%)
  between operations  15.1 us (5%)
  local copies, waits for them, and re-layouts  14.8 us (5%)
  starting transfers between devices  11.5 us (4%)
    all_to_all x1, waiting for transfers between devices, on_device(): lax.all_to_all(produced, 'ea', split_axis=0, concat_axis=0, tiled=True, a...  53.6 us
    reduce_scatter x1, waiting for transfers between devices, on_device(): lax.psum_scatter(partial.reshape(layers, tokens, width), 'ea', scatter_di...  43.5 us
    all_gather x1, waiting for transfers between devices, on_device(): full_weight = lax.all_gather(value_weight, 'ea', axis=0, tiled=True)  42.6 us
    all_gather x1, blocking collectives, on_device(): routes = lax.all_gather(route, 'ea', axis=0, axis_index_groups=across)  28.4 us
    ppermute x5, waiting for transfers between devices, shifted(): return lax.ppermute(field, 'sa', [(i, i + by) for i in range(n_sa - by)])  22.3 us
    dot_general x2, matrix products, mm(): lax.dot_general(a.astype(BF), b.astype(BF), (dims, ((), ())), preferred_e...  20.6 us
    pallas_call x1, Pallas kernels, prepare(): pl.pallas_call(lambda *refs: prepare_kernel(*refs, pairs=pairs), grid=(st...  11.9 us
    dot_general x1, matrix products, on_device(): jnp.einsum('perf,efd->perd', hidden, down_weight, preferred_element_type=...  9.54 us
  transfers between devices with their start and end apart: 8, of which 6 were waited for; matrix products, arithmetic and copies ran while one was open for 1% of the time, Pallas kernels for 8%

commit v1 on v0

--- a/solution.py
+++ b/solution.py
@@ -1,5 +1,8 @@
+import functools
+
 import jax
 import jax.numpy as jnp
+import numpy as np
 from jax import lax
 from jax.experimental import pallas as pl
 from jax.experimental.pallas import tpu as pltpu
@@ -11,6 +14,7 @@
 DV = 128
 BF = jnp.bfloat16
 F32 = jnp.float32
+MESH = pl.DeviceIdType.MESH
 
 
 def mm(a, b, dims=((1,), (0,))):
@@ -87,8 +91,10 @@
         last = g_col[n - 1 : n, :]
         ktail = kf * (kn_col * jnp.exp(last - g_col))
         a_ref[h] = (jnp.exp(last) * eye - mm(ktail, emat, ((0,), (0,)))).astype(BF)
-        mbo_ref[h, :n, :] = mm(scores, mix).astype(BF)
-        mbo_ref[h, n:, :] = mm(ktail, mix, ((0,), (0,))).astype(BF)
+        for at, part in ((0, mm3(scores, mix)), (n, mm3(jnp.transpose(ktail), mix))):
+            high = part.astype(BF)
+            mbo_ref[h, at : at + n, :] = high
+            mbo_ref[h, 2 * n + at : 3 * n + at, :] = (part - high.astype(F32)).astype(BF)
         g_ref[h] = (jnp.exp(g_col) * qn_col * qf - mm(scores, emat)).astype(BF)
 
 
@@ -109,12 +115,12 @@
             pl.BlockSpec((heads, n), lambda i: (i, 0)),
         ],
         out_specs=[
-            pl.BlockSpec((heads, 2 * n, n), lambda i: (i, 0, 0)),
+            pl.BlockSpec((heads, 4 * n, n), lambda i: (i, 0, 0)),
             pl.BlockSpec((heads, DK, DK), lambda i: (i, 0, 0)),
             pl.BlockSpec((heads, n, DK), lambda i: (i, 0, 0)),
         ],
         out_shape=[
-            jax.ShapeDtypeStruct((HV, 2 * n, n), BF),
+            jax.ShapeDtypeStruct((HV, 4 * n, n), BF),
             jax.ShapeDtypeStruct((HV, DK, DK), BF),
             jax.ShapeDtypeStruct((HV, n, DK), BF),
         ],
@@ -151,9 +157,10 @@
         scale = lax.rsqrt(jnp.mean(stream * stream, axis=-1, keepdims=True) + 1e-06)
         normed[...] = (stream * scale * gain_ref[...].astype(F32)).astype(BF)
 
-    values = mm(normed[...], w_ref[...]).astype(BF)
+    values = mm(normed[...], w_ref[0]).astype(BF)
     for h in range(mbo_ref.shape[0]):
         both = mm(mbo_ref[h], values[:, h * DV : (h + 1) * DV])
+        both = both[: 2 * n] + both[2 * n :]
         zero_ref[:, h * DV : (h + 1) * DV] = both[:n]
         b_ref[h] = both[n:].astype(BF)
 
@@ -168,8 +175,8 @@
             pl.BlockSpec((n, width), lambda i: (0, 0)),
             pl.BlockSpec((n, width), lambda i: (0, 0)),
             pl.BlockSpec((1, width), lambda i: (0, 0)),
-            pl.BlockSpec((width, heads * DV), lambda i: (0, i)),
-            pl.BlockSpec((heads, 2 * n, n), lambda i: (i, 0, 0)),
+            pl.BlockSpec((1, width, heads * DV), lambda i: (i, 0, 0)),
+            pl.BlockSpec((heads, 4 * n, n), lambda i: (i, 0, 0)),
         ],
         out_specs=[
             pl.BlockSpec((n, heads * DV), lambda i: (0, i)),
@@ -202,8 +209,245 @@
     )(zero, reached, b1, b2, b3)
 
 
+def exchange_kernel(
+    plane, layers, hid_ref, down_ref, order_ref, ids_ref, amount_ref, moe_ref,
+    hidden, outgoing, incoming, mixing, dense, zout, zin, routes,
+    xs, xr, zs, zr, rs, rr,
+):
+    exp_dev, rows, _ = hid_ref.shape
+    tokens, top = ids_ref.shape
+    chunks, _, block, wide = outgoing.shape
+    cap = rows // (plane * layers)
+    group = layers * cap
+    per_layer = plane * block
+    me = lax.axis_index("ea")
+    spot, layer = me % plane, me // plane
+    sign = 1 - 2 * (me % 2)
+    half = layers // 2
+
+    def device(z, p):
+        return {"ea": ((z + 2 * layers) % layers) * plane + p % plane}
+
+    barrier = pltpu.get_barrier_semaphore()
+    for r in range(1, plane):
+        pl.semaphore_signal(barrier, inc=1, device_id=device(layer, spot + r), device_id_type=MESH)
+    for r in range(1, layers):
+        pl.semaphore_signal(barrier, inc=1, device_id=device(layer + r, spot), device_id_type=MESH)
+    pl.semaphore_wait(barrier, plane + layers - 2)
+
+    experts = exp_dev * plane * layers
+    lane = lax.broadcasted_iota(jnp.int32, (tokens, experts), 1)
+    ids = ids_ref[...]
+    counts = jnp.zeros((tokens, experts), F32)
+    for i in range(top):
+        counts += jnp.where(lane == ids[:, i : i + 1], 1.0, 0.0)
+    trow = lax.broadcasted_iota(jnp.int32, (tokens, tokens), 0)
+    tcol = lax.broadcasted_iota(jnp.int32, (tokens, tokens), 1)
+    prior = mm(jnp.where(trow > tcol, 1.0, 0.0), counts)
+    place = (ids // exp_dev) * block + (ids % exp_dev) * group
+    columns = []
+    for i in range(top):
+        slot = jnp.sum(jnp.where(lane == ids[:, i : i + 1], prior, 0.0), axis=1, keepdims=True)
+        columns.append(place[:, i : i + 1].astype(F32) + slot)
+    columns += [amount_ref[:, i : i + 1] for i in range(top)]
+    table = jnp.zeros((tokens, 128), F32)
+    tl = lax.broadcasted_iota(jnp.int32, (tokens, 128), 1)
+    for i, column in enumerate(columns):
+        table = jnp.where(tl == i, column, table)
+    deep = routes.shape[1]
+    routes[layer] = jnp.transpose(table)[:deep]
+
+    for e in range(exp_dev):
+        hidden[e] = mm(order_ref[...], hid_ref[e]).astype(BF)
+
+    def route_copy(r):
+        return pltpu.make_async_remote_copy(
+            src_ref=routes.at[layer],
+            dst_ref=routes.at[layer],
+            send_sem=rs.at[r],
+            recv_sem=rr.at[r],
+            device_id=device(layer + r, spot),
+            device_id_type=MESH,
+        )
+
+    for r in range(1, layers):
+        route_copy(r).start()
+
+    def produce(c):
+        at = pl.ds(pl.multiple_of(c * wide, wide), wide)
+        made = [mm(hidden[e], down_ref[e, :, at]) for e in range(exp_dev)]
+        for p in range(plane):
+            mine = [m[p * group : (p + 1) * group] for m in made]
+            outgoing[c, p] = jnp.concatenate(mine, axis=0).astype(BF)
+
+    def ship(c):
+        for r in range(1, plane):
+            to = (spot + r) % plane
+            pltpu.make_async_remote_copy(
+                src_ref=outgoing.at[c, to],
+                dst_ref=incoming.at[c, spot],
+                send_sem=xs.at[c, r],
+                recv_sem=xr.at[c, r],
+                device_id=device(layer, to),
+                device_id_type=MESH,
+            ).start()
+        incoming[c, spot] = outgoing[c, spot]
+
+    produce(0)
+
+    @pl.loop(1, chunks)
+    def _(c):
+        produce(c)
+        ship(c - 1)
+
+    ship(chunks - 1)
+
+    for r in range(1, layers):
+        route_copy(r).wait_recv()
+
+    @pl.loop(0, layers)
+    def _(z):
+        table = jnp.concatenate([routes[z], jnp.zeros((128 - deep, tokens), F32)], axis=0)
+        table = jnp.transpose(table)
+        shift = (z * cap - layer * per_layer).astype(F32)
+        start = pl.ds(pl.multiple_of(z * tokens, tokens), tokens)
+        for k in range(per_layer // 256):
+            slot_of = (lax.broadcasted_iota(jnp.int32, (tokens, 256), 1) + k * 256).astype(F32)
+            total = jnp.zeros((tokens, 256), F32)
+            for i in range(top):
+                total += jnp.where(
+                    slot_of == table[:, i : i + 1] + shift, table[:, top + i : top + i + 1], 0.0
+                )
+            mixing[start, k * 256 : (k + 1) * 256] = total.astype(BF)
+
+    def hop(j, s):
+        ahead = s < half
+        step = s if ahead else s - half
+        way = sign if ahead else -sign
+        return pltpu.make_async_remote_copy(
+            src_ref=zout.at[j, s],
+            dst_ref=zin.at[j, s],
+            send_sem=zs.at[j, s],
+            recv_sem=zr.at[j, s],
+            device_id=device(layer + way, spot),
+            device_id_type=MESH,
+        )
+
+    def target(s):
+        if s < half:
+            return (layer + sign * (half - s) + 2 * layers) % layers
+        return (layer - sign * (half - 1 - (s - half)) + 2 * layers) % layers
+
+    hops = layers - 1
+
+    def stage(j, s):
+        sent = []
+        for h in (s, s + half):
+            if (h < half) == (h == s) and h < hops:
+                part = dense[j % 5, target(h)]
+                if s > 0:
+                    hop(j, h - 1).wait_recv()
+                    part = part + zin[j, h - 1].astype(F32)
+                zout[j, h] = part.astype(BF)
+                sent.append(h)
+        for h in sent:
+            hop(j, h).start()
+
+    @pl.loop(0, chunks + half)
+    def _(i):
+        @pl.when(i >= half)
+        def _():
+            j = i - half
+            hop(j, half - 1).wait_recv()
+            hop(j, hops - 1).wait_recv()
+            total = dense[j % 5, layer] + zin[j, half - 1].astype(F32) + zin[j, hops - 1].astype(F32)
+            moe_ref[:, pl.ds(pl.multiple_of(j * wide, wide), wide)] = total
+
+        for s in range(half - 1, 0, -1):
+            @pl.when((i >= s) & (i < chunks + s))
+            def _():
+                stage(i - s, s)
+
+        @pl.when(i < chunks)
+        def _():
+            for r in range(1, plane):
+                pltpu.make_async_remote_copy(
+                    src_ref=outgoing.at[i, spot],
+                    dst_ref=incoming.at[i, spot],
+                    send_sem=xs.at[i, r],
+                    recv_sem=xr.at[i, r],
+                    device_id=device(layer, spot + r),
+                    device_id_type=MESH,
+                ).wait_recv()
+            rowsin = incoming[i].reshape(per_layer, wide)
+            for z in range(layers):
+                dense[i % 5, z] = mm(mixing[z * tokens : (z + 1) * tokens, :], rowsin)
+            stage(i, 0)
+
+    for r in range(1, layers):
+        route_copy(r).wait_send()
+
+    @pl.loop(0, chunks)
+    def _(c):
+        for r in range(1, plane):
+            pltpu.make_async_remote_copy(
+                src_ref=outgoing.at[c, spot],
+                dst_ref=incoming.at[c, spot],
+                send_sem=xs.at[c, r],
+                recv_sem=xr.at[c, r],
+                device_id=device(layer, spot + r),
+                device_id_type=MESH,
+            ).wait_send()
+        for s in range(hops):
+            hop(c, s).wait_send()
+
+
+def exchange(plane, expert_hidden, down_weight, ids, amount):
+    exp_dev, rows, ff_units = expert_hidden.shape
+    width = down_weight.shape[2]
+    n_ea = lax.axis_size("ea")
+    layers = n_ea // plane
+    cap = rows // n_ea
+    tokens, top = ids.shape
+    wide = 256
+    chunks = width // wide
+    block = exp_dev * layers * cap
+    source = np.arange(rows).reshape(layers, plane, cap).transpose(1, 0, 2).reshape(-1)
+    order = np.zeros((rows, rows), np.float32)
+    order[np.arange(rows), source] = 1.0
+    vmem = pl.BlockSpec(memory_space=pltpu.VMEM)
+    dma = pltpu.SemaphoreType.DMA
+    return pl.pallas_call(
+        functools.partial(exchange_kernel, plane, layers),
+        out_shape=jax.ShapeDtypeStruct((tokens, width), F32),
+        in_specs=[vmem] * 5,
+        out_specs=vmem,
+        scratch_shapes=[
+            pltpu.VMEM((exp_dev, rows, ff_units), BF),
+            pltpu.VMEM((chunks, plane, block, wide), BF),
+            pltpu.VMEM((chunks, plane, block, wide), BF),
+            pltpu.VMEM((layers * tokens, plane * block), BF),
+            pltpu.VMEM((5, layers, tokens, wide), F32),
+            pltpu.VMEM((chunks, layers - 1, tokens, wide), BF),
+            pltpu.VMEM((chunks, layers - 1, tokens, wide), BF),
+            pltpu.VMEM((layers, 24, tokens), F32),
+            dma((chunks, plane)),
+            dma((chunks, plane)),
+            dma((chunks, layers - 1)),
+            dma((chunks, layers - 1)),
+            dma((layers,)),
+            dma((layers,)),
+        ],
+        compiler_params=pltpu.CompilerParams(
+            collective_id=0, has_side_effects=True, vmem_limit_bytes=60 * 1024 * 1024
+        ),
+        cost_estimate=pl.CostEstimate(flops=60_000_000_000, bytes_accessed=12_000_000, transcendentals=0),
+        name="exchange",
+    )(expert_hidden, down_weight, jnp.asarray(order, BF), ids, amount)
+
+
 def on_device(
-    shape_x,
+    plane,
     expert_hidden,
     down_weight,
     residual,
@@ -216,55 +460,8 @@
     log_decay,
     write_rate,
 ):
-    n_ea = lax.axis_size("ea")
     n_sa = lax.axis_size("sa")
-    exp_dev, ff_units, width = down_weight.shape
-    cap = expert_hidden.shape[1] // n_ea
-    experts = exp_dev * n_ea
-    tokens = residual.shape[1]
-    top = expert_ids.shape[2]
-    plane = shape_x
-    layers = n_ea // plane
-    in_plane = [[z * plane + i for i in range(plane)] for z in range(layers)]
-    across = [[z * plane + i for z in range(layers)] for i in range(plane)]
-    me = lax.axis_index("ea")
-    my_layer = me // plane
-
-    hidden = expert_hidden.reshape(exp_dev, layers, plane, cap, ff_units).transpose(2, 0, 1, 3, 4)
-    hidden = hidden.reshape(plane, exp_dev, layers * cap, ff_units)
-    produced = jnp.einsum("perf,efd->perd", hidden, down_weight, preferred_element_type=F32).astype(BF)
-    received = lax.all_to_all(
-        produced, "ea", split_axis=0, concat_axis=0, tiled=True, axis_index_groups=in_plane
-    )
-    per_layer = plane * exp_dev * layers * cap
-    received = received.reshape(per_layer, width)
-
-    ids = expert_ids[0]
-    onehot = ids[:, :, None] == jnp.arange(experts, dtype=jnp.int32)[None, None, :]
-    counts = jnp.sum(onehot.astype(F32), axis=1)
-    earlier = lax.broadcasted_iota(jnp.int32, (tokens, tokens), 0) > lax.broadcasted_iota(
-        jnp.int32, (tokens, tokens), 1
-    )
-    prior = mm(earlier, counts)
-    slots = jnp.sum(jnp.where(onehot, prior[:, None, :], 0.0), axis=-1)
-    place = (ids // exp_dev) * (exp_dev * layers * cap) + (ids % exp_dev) * (layers * cap)
-    route = jnp.concatenate([place.astype(F32) + slots, combine_weight[0]], axis=1)
-    routes = lax.all_gather(route, "ea", axis=0, axis_index_groups=across)
-    offset = (jnp.arange(layers) * cap - my_layer * per_layer).astype(F32)[:, None, None]
-    where_to = (routes[:, :, :top] + offset).reshape(layers * tokens, top).astype(jnp.int32)
-    amount = routes[:, :, top:].reshape(layers * tokens, top)
-    slot_of = lax.broadcasted_iota(jnp.int32, (layers * tokens, per_layer), 1)
-    mixing = jnp.zeros((layers * tokens, per_layer), F32)
-    for i in range(top):
-        mixing = mixing + jnp.where(slot_of == where_to[:, i : i + 1], amount[:, i : i + 1], 0.0)
-    partial = mm(mixing, received).astype(BF)
-    moe = lax.psum_scatter(
-        partial.reshape(layers, tokens, width),
-        "ea",
-        scatter_dimension=0,
-        axis_index_groups=across,
-        tiled=False,
-    )
+    moe = exchange(plane, expert_hidden, down_weight, expert_ids[0], combine_weight[0])
 
     summed = jnp.cumsum(log_decay[0], axis=0)
     mbo, amat, gmat = prepare(queries[0], keys[0], summed, write_rate[0])
@@ -273,7 +470,10 @@
         return lax.ppermute(field, "sa", [(i, i + by) for i in range(n_sa - by)])
 
     reached = reach(gmat, shifted(amat, 1), shifted(amat, 2))
-    full_weight = lax.all_gather(value_weight, "ea", axis=0, tiled=True)
+    share = value_weight.shape[1] // n_sa
+    strip = lax.dynamic_slice_in_dim(value_weight, lax.axis_index("sa") * share, share, axis=1)
+    strip = lax.all_gather(strip, "ea", axis=0, tiled=True)
+    full_weight = lax.all_gather(strip, "sa", axis=0)
     zero, bmat = project(moe, residual[0], norm_gain, full_weight, mbo)
     out = finish(zero, reached, shifted(bmat, 1), shifted(bmat, 2), shifted(bmat, 3))
     return out[None]

time: 290 us -> 269 us (0.928)
  Pallas kernels: 25.5 us -> 137 us
  waiting for transfers between devices: 163 us -> 102 us
  matrix products: 30.1 us -> 0 us
  blocking collectives: 28.4 us -> 0 us
  local copies, waits for them, and re-layouts: 14.8 us -> 7.17 us
  starting transfers between devices: 11.5 us -> 6.67 us
    pallas_call x0 -> x1, Pallas kernels: none -> 110 us  [exchange(): pl.pallas_call(functools.partial(exchange_kernel, plane, layers), out_sha...]
    all_to_all x1 -> x0, waiting for transfers between devices: 53.6 us -> none  [on_device(): lax.all_to_all(produced, 'ea', split_axis=0, concat_axis=0, tiled=True, a...]
    reduce_scatter x1 -> x0, waiting for transfers between devices: 43.5 us -> none  [on_device(): lax.psum_scatter(partial.reshape(layers, tokens, width), 'ea', scatter_di...]
    all_gather x1 -> x2, waiting for transfers between devices: 42.6 us -> 82 us  [the longest x1 82 us: on_device(): strip = lax.all_gather(strip, 'ea', axis=0, tiled=True)]
    dot_general x3 -> x0, matrix products: 30.1 us -> none  [the longest x2 20.6 us: mm(): lax.dot_general(a.astype(BF), b.astype(BF), (dims, ((), ())), preferred_e...]
    all_gather x1 -> x0, blocking collectives: 28.4 us -> none  [on_device(): routes = lax.all_gather(route, 'ea', axis=0, axis_index_groups=across)]
    convert_element_type x1 -> x0, local copies, waits for them, and re-layouts: 7.49 us -> none  [on_device(): jnp.einsum('perf,efd->perd', hidden, down_weight, preferred_element_type=...]
    all_to_all x1 -> x0, starting transfers between devices: 4.96 us -> none  [on_device(): lax.all_to_all(produced, 'ea', split_axis=0, concat_axis=0, tiled=True, a...]
  transfers between devices with their start and end apart: 8 -> 7, of which waited for: 6 -> 2; matrix products, arithmetic and copies ran while one was open for 1% -> 1% of each run, Pallas kernels for 8% -> 50%
where the time goes in v1:
time: 269 us; the launch traced here: 267 us
  Pallas kernels  137 us (51%)
  waiting for transfers between devices  102 us (38%)
  between operations  13.5 us (5%)
  local copies, waits for them, and re-layouts  7.17 us (3%)
  starting transfers between devices  6.67 us (2%)
    pallas_call x1, Pallas kernels, exchange(): pl.pallas_call(functools.partial(exchange_kernel, plane, layers), out_sha...  110 us
    all_gather x1, waiting for transfers between devices, on_device(): strip = lax.all_gather(strip, 'ea', axis=0, tiled=True)  82 us
    ppermute x5, waiting for transfers between devices, shifted(): return lax.ppermute(field, 'sa', [(i, i + by) for i in range(n_sa - by)])  20.4 us
    pallas_call x1, Pallas kernels, prepare(): pl.pallas_call(lambda *refs: prepare_kernel(*refs, pairs=pairs), grid=(st...  12.7 us
    pallas_call x1, Pallas kernels, project(): pl.pallas_call(values_kernel, grid=(HV // heads,), in_specs=[pl.BlockSpec...  7.52 us
    ppermute x5, starting transfers between devices, shifted(): return lax.ppermute(field, 'sa', [(i, i + by) for i in range(n_sa - by)])  6.62 us
  transfers between devices with their start and end apart: 7, of which 2 were waited for; matrix products, arithmetic and copies ran while one was open for 1% of the time, Pallas kernels for 50%

profile of v1, /device:TPU:24, one launch (start us, length us, event | category | flops | bytes accessed | tf_op | source)
XLA Modules:
  0.0 266.8 jit_solution(2902226340344671971)
XLA Ops:
  6.5 0.0 copy-start
  6.5 0.0 copy-start.7
  6.5 0.0 copy-start.8
  6.5 0.0 all-gather.4.cloned.1.call-start
  6.6 0.9 copy-done
  7.4 0.6 constant_dynamic-slice_fusion
  8.1 0.0 all-gather.4.cloned.1.call-update
  8.1 0.0 all-gather.6.cloned.1.call-start
  8.1 82.0 %all-gather.4.cloned.1.call-done = bf16[2048,512]{1,0:T(8,128)(2,1)} async-done(((bf16[32,512]{1,0:T(8,128)(2,1)}), bf16[2048,512]{1,0:T(8,128)(2,1)}) %all-gather.4.cloned.1.call-update) | async-done | bytes 2097168 | tf_op jit(solution)/shard_map/all_gather | solution.py:475
  90.1 0.0 all-gather.6.cloned.1.call-update
  90.2 0.0 copy-done.7
  90.2 0.1 copy.15
  90.3 0.2 reduce_window_sum.11.refs_2_
  90.4 0.0 copy-start.6
  90.4 0.7 copy.16
  91.1 0.0 copy-done.8
  91.1 0.7 copy.17.refs_3_
  91.8 0.0 copy-done.6
  91.8 0.0 copy-start.11
  91.8 0.0 copy-start.9
  91.9 0.0 copy-start.10
  91.9 12.7 %prepare.1 = (bf16[16,512,128]{2,1,0:T(8,128)(2,1)}, bf16[16,128,128]{2,1,0:T(8,128)(2,1)}, bf16[16,128,128]{2,1,0:T(8,128)(2,1)}) custom-call(bf16[128,1024]{1,0:T(8,128)(2,1)} %bitcast.20, bf16[128,1024]{1,0:T(8,128)(2,1)} %bitcast.21, f32[128,16]{1,0:T(8,128)} %copy-done.6, f32[128,16]{1,0:T(8,128)} %copy.17.refs_3_, f32[16,128]{1,0:T(8,128)} %bitcast.19, ...), custom_call_target="tpu_custom_call" | custom-call | flops 4000000000 | bytes 4000000 | tf_op jit(solution)/shard_map/prepare/pallas_call | solution.py:106
  104.6 1.3 collective-permute-start.1
  105.9 1.5 collective-permute-start
  107.3 0.0 copy-done.11
  107.4 0.6 reshape.3.gain_ref
  108.0 0.0 copy-done.9
  108.0 0.7 copy.13
  108.7 0.0 copy-done.10
  108.7 0.7 copy.14
  109.4 110.0 %exchange.1.moe_ref = f32[128,2048]{1,0:T(8,128)} custom-call(bf16[4,448,512]{2,1,0:T(8,128)(2,1)} %hid_ref.1, bf16[4,512,2048]{2,1,0:T(8,128)(2,1)} %down_ref.1, bf16[448,448]{1,0:T(8,128)(2,1)} %constant.16.clone.order_ref, s32[128,10]{1,0:T(8,128)} %bitcast.14, f32[128,10]{1,0:T(8,128)} %bitcast.15), custom_call_target="tpu_custom_call" | custom-call | flops 60000002048 | bytes 12000000 | tf_op jit(solution)/shard_map/exchange/pallas_call | solution.py:420
  219.5 0.0 all-gather.6.cloned.1.call-done
  219.5 7.5 %project.1 = (f32[128,2048]{1,0:T(8,128)}, bf16[16,128,128]{2,1,0:T(8,128)(2,1)}) custom-call(f32[128,2048]{1,0:T(8,128)} %exchange.1.moe_ref, bf16[128,2048]{1,0:T(8,128)(2,1)} %bitcast.13, bf16[1,2048]{1,0:T(2,128)(2,1)} %reshape.3.gain_ref, bf16[4,2048,512]{2,1,0:T(8,128)(2,1)} %bitcast.12, bf16[16,512,128]{2,1,0:T(8,128)(2,1)} %get-tuple-element.10.mbo_ref), custom_call_target="tpu_custom_call" | custom-call | flops 1200000000 | bytes 12000000 | tf_op jit(solution)/shard_map/project/pallas_call | solution.py:171
  227.0 1.3 collective-permute-start.4
  228.3 1.3 collective-permute-start.3
  229.6 1.3 collective-permute-start.2
  230.9 0.0 collective-permute-done.1.a2_ref
  230.9 0.0 copy-start.4
  230.9 0.0 collective-permute-done.a1_ref
  230.9 0.0 copy-start.5
  231.0 0.8 copy-done.4
  231.8 0.1 copy-done.5
  231.9 3.0 %reach.1.reach_ref = bf16[16,128,384]{2,1,0:T(8,128)(2,1)} custom-call(bf16[16,128,128]{2,1,0:T(8,128)(2,1)} %get-tuple-element.12.g_ref, bf16[16,128,128]{2,1,0:T(8,128)(2,1)} %copy-done.5, bf16[16,128,128]{2,1,0:T(8,128)(2,1)} %copy-done.4), custom_call_target="tpu_custom_call" | custom-call | flops 200000000 | bytes 4000000 | tf_op jit(solution)/shard_map/reach/pallas_call | solution.py:143
  234.9 20.4 %collective-permute-done.4.b3_ref = bf16[16,128,128]{2,1,0:T(8,128)(2,1)S(1)} collective-permute-done((bf16[16,128,128]{2,1,0:T(8,128)(2,1)}, bf16[16,128,128]{2,1,0:T(8,128)(2,1)S(1)}, u32[]{:S(2)}, u32[]{:S(2)}) %collective-permute-start.4) | collective-permute-done | bytes 524320 | tf_op jit(solution)/shard_map/ppermute | solution.py:470
  255.3 0.0 copy-start.1
  255.3 0.0 collective-permute-done.3.b2_ref
  255.3 0.0 copy-start.2
  255.3 0.0 collective-permute-done.2.b1_ref
  255.3 0.0 copy-start.3
  255.3 0.8 copy-done.1
  256.1 0.2 copy-done.2
  256.3 0.2 copy-done.3
  256.5 3.5 %finish.1 = bf16[128,2048]{1,0:T(8,128)(2,1)} custom-call(f32[128,2048]{1,0:T(8,128)} %get-tuple-element.11.zero_ref, bf16[16,128,384]{2,1,0:T(8,128)(2,1)} %reach.1.reach_ref, bf16[16,128,128]{2,1,0:T(8,128)(2,1)} %copy-done.3, bf16[16,128,128]{2,1,0:T(8,128)(2,1)} %copy-done.2, bf16[16,128,128]{2,1,0:T(8,128)(2,1)} %copy-done.1), custom_call_target="tpu_custom_call" | custom-call | tf_op jit(solution)/shard_map/finish/pallas_call | solution.py:205
Async XLA Ops:
  6.5 0.9 copy-start
  6.5 83.6 %copy-start.7 = (f32[1,128,16]{1,2,0:T(8,128)S(1)}, f32[1,128,16]{1,2,0:T(8,128)}, u32[]{:S(2)}) copy-start(f32[1,128,16]{1,2,0:T(8,128)} %param.21) | copy-start | bytes 24580
  6.5 84.6 %copy-start.8 = (f32[1,128,16]{1,2,0:T(8,128)S(1)}, f32[1,128,16]{1,2,0:T(8,128)}, u32[]{:S(2)}) copy-start(f32[1,128,16]{1,2,0:T(8,128)} %param.22) | copy-start | bytes 24580
  6.5 83.6 %all-gather.4.cloned.1.call-start = ((), (), s32[]{:S(2)}) async-start(), calls=%async_computation | async-start | bytes 2129920 | tf_op jit(solution)/shard_map/all_gather | solution.py:475
  8.1 211.4 %all-gather.6.cloned.1.call-start = ((), (), s32[]{:S(2)}) async-start(), calls=%async_computation.1 | async-start | bytes 10485760 | tf_op jit(solution)/shard_map/all_gather | solution.py:476
  90.4 1.4 copy-start.6
  91.8 15.5 %copy-start.11 = (bf16[2048]{0:T(1024)(128)(2,1)S(1)}, bf16[2048]{0:T(1024)(128)(2,1)}, u32[]{:S(2)}) copy-start(bf16[2048]{0:T(1024)(128)(2,1)} %param.17) | copy-start | bytes 12292
  91.8 16.1 %copy-start.9 = (s32[1,128,10]{1,0,2:T(1,128)S(1)}, s32[1,128,10]{1,0,2:T(1,128)}, u32[]{:S(2)}) copy-start(s32[1,128,10]{1,0,2:T(1,128)} %param.15) | copy-start | bytes 15364
  91.9 16.8 %copy-start.10 = (f32[1,128,10]{1,0,2:T(1,128)S(1)}, f32[1,128,10]{1,0,2:T(1,128)}, u32[]{:S(2)}) copy-start(f32[1,128,10]{1,0,2:T(1,128)} %param.16) | copy-start | bytes 15364
  104.6 126.3 %collective-permute-start.1 = (bf16[16,128,128]{2,1,0:T(8,128)(2,1)}, bf16[16,128,128]{2,1,0:T(8,128)(2,1)S(1)}, u32[]{:S(2)}, u32[]{:S(2)}) collective-permute-start(bf16[16,128,128]{2,1,0:T(8,128)(2,1)} %get-tuple-element.13), channel_id=1, source_target_pairs={{0,2},{1,3},{4,6},{5,7},{8,10},{9,11},{12,14},{13,15},{16,18},{17,... | collective-permute-start | bytes 1572872 | tf_op jit(solution)/shard_map/ppermute | solution.py:470
  105.9 125.1 %collective-permute-start = (bf16[16,128,128]{2,1,0:T(8,128)(2,1)}, bf16[16,128,128]{2,1,0:T(8,128)(2,1)S(1)}, u32[]{:S(2)}, u32[]{:S(2)}) collective-permute-start(bf16[16,128,128]{2,1,0:T(8,128)(2,1)} %get-tuple-element.13), channel_id=1, source_target_pairs={{0,1},{1,2},{2,3},{4,5},{5,6},{6,7},{8,9},{9,10},{10,11},{12,13},{... | collective-permute-start | bytes 1572872 | tf_op jit(solution)/shard_map/ppermute | solution.py:470
  227.0 28.3 %collective-permute-start.4 = (bf16[16,128,128]{2,1,0:T(8,128)(2,1)}, bf16[16,128,128]{2,1,0:T(8,128)(2,1)S(1)}, u32[]{:S(2)}, u32[]{:S(2)}) collective-permute-start(bf16[16,128,128]{2,1,0:T(8,128)(2,1)} %get-tuple-element.14), channel_id=1, source_target_pairs={{0,3},{4,7},{8,11},{12,15},{16,19},{20,23},{24,27},{28,31},{32,35}... | collective-permute-start | bytes 1572872 | tf_op jit(solution)/shard_map/ppermute | solution.py:470
  228.3 27.0 %collective-permute-start.3 = (bf16[16,128,128]{2,1,0:T(8,128)(2,1)}, bf16[16,128,128]{2,1,0:T(8,128)(2,1)S(1)}, u32[]{:S(2)}, u32[]{:S(2)}) collective-permute-start(bf16[16,128,128]{2,1,0:T(8,128)(2,1)} %get-tuple-element.14), channel_id=1, source_target_pairs={{0,2},{1,3},{4,6},{5,7},{8,10},{9,11},{12,14},{13,15},{16,18},{17,... | collective-permute-start | bytes 1572872 | tf_op jit(solution)/shard_map/ppermute | solution.py:470
  229.6 25.7 %collective-permute-start.2 = (bf16[16,128,128]{2,1,0:T(8,128)(2,1)}, bf16[16,128,128]{2,1,0:T(8,128)(2,1)S(1)}, u32[]{:S(2)}, u32[]{:S(2)}) collective-permute-start(bf16[16,128,128]{2,1,0:T(8,128)(2,1)} %get-tuple-element.14), channel_id=1, source_target_pairs={{0,1},{1,2},{2,3},{4,5},{5,6},{6,7},{8,9},{9,10},{10,11},{12,13},{... | collective-permute-start | bytes 1572872 | tf_op jit(solution)/shard_map/ppermute | solution.py:470
  230.9 0.8 copy-start.4
  230.9 0.9 copy-start.5
  255.3 0.8 copy-start.1
  255.3 1.0 copy-start.2
  255.3 1.1 copy-start.3
Sparse Core Ops, SparseCore 0:
  10.1 79.9 all-gather.3
  91.9 93.2 all-gather.5

commit v2 on v1

v2 whole, which is shorter than its diff:
```python
import functools

import jax
import jax.numpy as jnp
import numpy as np
from jax import lax
from jax.experimental import pallas as pl
from jax.experimental.pallas import tpu as pltpu
from jax.sharding import PartitionSpec as P

HV = 16
HK = 8
DK = 128
DV = 128
BF = jnp.bfloat16
F32 = jnp.float32
MESH = pl.DeviceIdType.MESH


def mm(a, b, dims=((1,), (0,))):
    return lax.dot_general(a.astype(BF), b.astype(BF), (dims, ((), ())), preferred_element_type=F32)


def mm_full(a, b, dims=((1,), (0,))):
    return lax.dot_general(
        a, b, (dims, ((), ())), preferred_element_type=F32, precision=lax.Precision.HIGHEST
    )


def mm3(a, b):
    ah, bh = a.astype(BF), b.astype(BF)
    al = (a - ah.astype(F32)).astype(BF)
    bl = (b - bh.astype(F32)).astype(BF)
    return mm(ah, bh) + (mm(ah, bl) + mm(al, bh))


def unit_lower_inverses(lowers):
    n = lowers[0].shape[0]
    row = lax.broadcasted_iota(jnp.int32, (n, n), 0)
    col = lax.broadcasted_iota(jnp.int32, (n, n), 1)
    eye = (row == col).astype(F32)
    size = 16
    same = (row // size) == (col // size)
    powers = [jnp.where(same, -low, 0.0) for low in lowers]
    outs = [eye + p for p in powers]
    for _ in range(3):
        powers = [mm3(p, p) for p in powers]
        outs = [o + mm3(p, o) for p, o in zip(powers, outs)]
    while size < n:
        join = ((row // (2 * size)) == (col // (2 * size))) & ((row // size) > (col // size))
        parts = [mm3(jnp.where(join, low, 0.0), o) for low, o in zip(lowers, outs)]
        outs = [o - mm3(o, p) for o, p in zip(outs, parts)]
        size *= 2
    return outs


PAIRS = 4


def gates(decay_ref, rate_ref, gate):
    n, heads = decay_ref.shape
    row = lax.broadcasted_iota(jnp.int32, (n, n), 0)
    col = lax.broadcasted_iota(jnp.int32, (n, n), 1)
    blank = jnp.zeros((n, n - heads), F32)
    summed = mm_full(
        jnp.where(row >= col, 1.0, 0.0), jnp.concatenate([decay_ref[...], blank], axis=1)
    )
    gate[0] = summed
    gate[1] = jnp.transpose(summed)
    gate[2] = jnp.concatenate([rate_ref[...], blank], axis=1)
    gate[3] = jnp.transpose(jnp.concatenate([rate_ref[...], blank], axis=1))


def prepare_heads(step, q_ref, k_ref, gate, mbo_ref, a_ref, g_ref):
    pairs = PAIRS
    n = q_ref.shape[0]
    row = lax.broadcasted_iota(jnp.int32, (n, n), 0)
    col = lax.broadcasted_iota(jnp.int32, (n, n), 1)
    inclusive = row >= col
    strict = row > col
    eye = (row == col).astype(F32)
    ones = jnp.ones((8, DK), F32)
    base = step * (2 * pairs)
    heads, lowers = [], []
    wide = pl.ds(pl.multiple_of(step * (pairs * DK), pairs * DK), pairs * DK)
    all_q, all_k = q_ref[:, wide], k_ref[:, wide]
    these = pl.ds(pl.multiple_of(base, 2 * pairs), 2 * pairs)
    sum_rows, rate_rows = gate[1, these], gate[3, these]
    for pair in range(pairs):
        q = all_q[:, pair * DK : (pair + 1) * DK]
        k = all_k[:, pair * DK : (pair + 1) * DK]
        qf, kf = q.astype(F32), k.astype(F32)
        kn_col = lax.rsqrt(jnp.sum(kf * kf, axis=-1, keepdims=True) + 1e-06)
        qn_col = lax.rsqrt(jnp.sum(qf * qf, axis=-1, keepdims=True) + 1e-06) * DK ** (-0.5)
        kn_row = lax.rsqrt(mm_full(ones, kf * kf, ((1,), (1,)))[:1] + 1e-06)
        kk = mm(k, k, ((1,), (1,))) * kn_col * kn_row
        qk = mm(q, k, ((1,), (1,))) * qn_col * kn_row
        for half in range(2):
            h = 2 * pair + half
            pick = col == base + h
            g_col = jnp.sum(jnp.where(pick, gate[0], 0.0), axis=1, keepdims=True)
            rate_col = jnp.sum(jnp.where(pick, gate[2], 0.0), axis=1, keepdims=True)
            g_row = sum_rows[h : h + 1, :]
            rate_row = rate_rows[h : h + 1, :]
            ratio = jnp.where(inclusive, jnp.exp(jnp.where(inclusive, g_col - g_row, 0.0)), 0.0)
            lowers.append(jnp.where(strict, rate_col * ratio * kk, 0.0))
            heads.append((h, q, k, qf, kf, kn_col, qn_col, kn_row, g_col, g_row, rate_row, qk * ratio))
    inverses = unit_lower_inverses(lowers)
    for inverse, (h, q, k, qf, kf, kn_col, qn_col, kn_row, g_col, g_row, rate_row, scores) in zip(inverses, heads):
        mix = inverse * rate_row
        emat = mm(mix * (jnp.exp(g_row) * kn_row), k)
        last = g_col[n - 1 : n, :]
        ktail = kf * (kn_col * jnp.exp(last - g_col))
        a_ref[base + h] = (jnp.exp(last) * eye - mm(ktail, emat, ((0,), (0,)))).astype(BF)
        for at, part in ((0, mm3(scores, mix)), (n, mm3(jnp.transpose(ktail), mix))):
            high = part.astype(BF)
            mbo_ref[base + h, at : at + n, :] = high
            mbo_ref[base + h, 2 * n + at : 3 * n + at, :] = (part - high.astype(F32)).astype(BF)
        g_ref[base + h] = (jnp.exp(g_col) * qn_col * qf - mm(scores, emat)).astype(BF)


def layer_kernel(
    plane, layers, hid_ref, down_ref, order_ref, ids_ref, amount_ref, res_ref, gain_ref, value_ref,
    q_ref, k_ref, decay_ref, rate_ref, out_ref,
    hidden, down, outgoing, incoming, mixing, dense, zout, zin, routes, moe,
    weight, mbo, amat, gmat, gate, fresh, later, earlier,
    dsem, xs, xr, zs, zr, rs, rr, ws, wr, ss, sr,
):
    exp_dev, rows, _ = hid_ref.shape
    tokens, top = ids_ref.shape
    chunks, _, block, wide = outgoing.shape
    cap = rows // (plane * layers)
    group = layers * cap
    per_layer = plane * block
    me = lax.axis_index("ea")
    spot, layer = me % plane, me // plane
    sign = 1 - 2 * (me % 2)
    half = layers // 2

    y = lax.axis_index("sa")
    n_sa = lax.axis_size("sa")
    core = me % 2
    strip = y * 2 + core
    near = spot // 2

    def chunk_copy(c):
        at = pl.ds(pl.multiple_of(c * wide, wide), wide)
        return pltpu.make_async_copy(down_ref.at[:, :, at], down.at[c % depth], dsem.at[c % depth])

    depth = down.shape[0]
    for c in range(depth):
        chunk_copy(c).start()

    def device(z, p):
        return {"ea": ((z + 2 * layers) % layers) * plane + p % plane}

    barrier = pltpu.get_barrier_semaphore()
    for r in range(1, plane):
        pl.semaphore_signal(barrier, inc=1, device_id=device(layer, spot + r), device_id_type=MESH)
    for r in range(1, layers):
        pl.semaphore_signal(barrier, inc=1, device_id=device(layer + r, spot), device_id_type=MESH)
    for r in range(1, n_sa):
        pl.semaphore_signal(barrier, inc=1, device_id={"sa": (y + r) % n_sa}, device_id_type=MESH)
    pl.semaphore_wait(barrier, plane + layers + n_sa - 3)

    own_rows, part = value_ref.shape[0], weight.shape[2]

    def remote(src, dst, at, to):
        return pltpu.make_async_remote_copy(
            src_ref=src, dst_ref=dst, send_sem=ws.at[at], recv_sem=wr.at[at],
            device_id=to, device_id_type=MESH,
        )

    def weight_rows(start, size):
        return weight.at[strip, pl.ds(pl.multiple_of(start * size, size), size)]

    def copy_beside():
        other = y * 2 + 1 - core
        cols = pl.ds(pl.multiple_of(other * part, part), part)
        mine = pl.ds(pl.multiple_of(me * own_rows, own_rows), own_rows)
        return remote(value_ref.at[:, cols], weight.at[other, mine], 0, {"ea": me + 1 - 2 * core})

    def copy_x(r):
        ref = weight_rows(me // 2, 2 * own_rows)
        return remote(ref, ref, r, device(layer, ((near + r) % (plane // 2)) * 2 + core))

    def copy_z(r):
        ref = weight_rows(layer, plane * own_rows)
        return remote(ref, ref, 3 + r, device(layer + r, spot))

    def copy_y(r):
        return remote(weight.at[strip], weight.at[strip], 10 + r, {"sa": (y + r) % n_sa})

    def copy_last(q):
        ref = weight.at[((y + q) % n_sa) * 2 + core]
        return remote(ref, ref, 14 + (y + q) % n_sa, {"ea": me + 1 - 2 * core})

    def landed(q):
        ref = weight.at[((y + q) % n_sa) * 2 + 1 - core]
        return remote(ref, ref, 14 + (y + q) % n_sa, {"ea": me + 1 - 2 * core})

    copy_beside().start()
    weight[strip, pl.ds(pl.multiple_of(me * own_rows, own_rows), own_rows)] = value_ref[
        :, pl.ds(pl.multiple_of(strip * part, part), part)
    ]

    experts = exp_dev * plane * layers
    lane = lax.broadcasted_iota(jnp.int32, (tokens, experts), 1)
    ids = ids_ref[...]
    counts = jnp.zeros((tokens, experts), F32)
    for i in range(top):
        counts += jnp.where(lane == ids[:, i : i + 1], 1.0, 0.0)
    trow = lax.broadcasted_iota(jnp.int32, (tokens, tokens), 0)
    tcol = lax.broadcasted_iota(jnp.int32, (tokens, tokens), 1)
    prior = mm(jnp.where(trow > tcol, 1.0, 0.0), counts)
    place = (ids // exp_dev) * block + (ids % exp_dev) * group
    columns = []
    for i in range(top):
        slot = jnp.sum(jnp.where(lane == ids[:, i : i + 1], prior, 0.0), axis=1, keepdims=True)
        columns.append(place[:, i : i + 1].astype(F32) + slot)
    columns += [amount_ref[:, i : i + 1] for i in range(top)]
    table = jnp.zeros((tokens, 128), F32)
    tl = lax.broadcasted_iota(jnp.int32, (tokens, 128), 1)
    for i, column in enumerate(columns):
        table = jnp.where(tl == i, column, table)
    deep = routes.shape[1]
    routes[layer] = jnp.transpose(table)[:deep]

    for e in range(exp_dev):
        hidden[e] = mm(order_ref[...], hid_ref[e]).astype(BF)

    def route_copy(r):
        return pltpu.make_async_remote_copy(
            src_ref=routes.at[layer],
            dst_ref=routes.at[layer],
            send_sem=rs.at[r],
            recv_sem=rr.at[r],
            device_id=device(layer + r, spot),
            device_id_type=MESH,
        )

    for r in range(1, layers):
        route_copy(r).start()

    copy_beside().wait_recv()
    for r in range(1, plane // 2):
        copy_x(r).start()

    def produce(c):
        chunk_copy(c).wait()
        made = [mm(hidden[e], down[c % depth, e]) for e in range(exp_dev)]
        for p in range(plane):
            mine = [m[p * group : (p + 1) * group] for m in made]
            outgoing[c, p] = jnp.concatenate(mine, axis=0).astype(BF)

        @pl.when(c + depth < chunks)
        def _():
            chunk_copy(c + depth).start()

    def ship(c):
        for r in range(1, plane):
            to = (spot + r) % plane
            pltpu.make_async_remote_copy(
                src_ref=outgoing.at[c, to],
                dst_ref=incoming.at[c, spot],
                send_sem=xs.at[c, r],
                recv_sem=xr.at[c, r],
                device_id=device(layer, to),
                device_id_type=MESH,
            ).start()
        incoming[c, spot] = outgoing[c, spot]

    produce(0)

    @pl.loop(1, chunks)
    def _(c):
        produce(c)
        ship(c - 1)

    ship(chunks - 1)

    for r in range(1, plane // 2):
        copy_x(r).wait_recv()
    for r in range(1, layers):
        copy_z(r).start()
    for r in range(1, layers):
        route_copy(r).wait_recv()

    @pl.loop(0, layers)
    def _(z):
        table = jnp.concatenate([routes[z], jnp.zeros((128 - deep, tokens), F32)], axis=0)
        table = jnp.transpose(table)
        shift = (z * cap - layer * per_layer).astype(F32)
        start = pl.ds(pl.multiple_of(z * tokens, tokens), tokens)
        for k in range(per_layer // 256):
            slot_of = (lax.broadcasted_iota(jnp.int32, (tokens, 256), 1) + k * 256).astype(F32)
            total = jnp.zeros((tokens, 256), F32)
            for i in range(top):
                total += jnp.where(
                    slot_of == table[:, i : i + 1] + shift, table[:, top + i : top + i + 1], 0.0
                )
            mixing[start, k * 256 : (k + 1) * 256] = total.astype(BF)

    gates(decay_ref, rate_ref, gate)
    prepare_heads(0, q_ref, k_ref, gate, mbo, amat, gmat)
    for r in range(1, layers):
        copy_z(r).wait_recv()
    for r in range(1, n_sa):
        copy_y(r).start()
    copy_last(0).start()

    @pl.loop(1, HK // PAIRS)
    def _(step):
        prepare_heads(step, q_ref, k_ref, gate, mbo, amat, gmat)

    def hop(j, s):
        ahead = s < half
        step = s if ahead else s - half
        way = sign if ahead else -sign
        return pltpu.make_async_remote_copy(
            src_ref=zout.at[j, s],
            dst_ref=zin.at[j, s],
            send_sem=zs.at[j, s],
            recv_sem=zr.at[j, s],
            device_id=device(layer + way, spot),
            device_id_type=MESH,
        )

    def target(s):
        if s < half:
            return (layer + sign * (half - s) + 2 * layers) % layers
        return (layer - sign * (half - 1 - (s - half)) + 2 * layers) % layers

    hops = layers - 1

    def stage(j, s):
        sent = []
        for h in (s, s + half):
            if (h < half) == (h == s) and h < hops:
                part = dense[j % 5, target(h)]
                if s > 0:
                    hop(j, h - 1).wait_recv()
                    part = part + zin[j, h - 1].astype(F32)
                zout[j, h] = part.astype(BF)
                sent.append(h)
        for h in sent:
            hop(j, h).start()

    @pl.loop(0, chunks + half)
    def _(i):
        @pl.when(i >= half)
        def _():
            j = i - half
            hop(j, half - 1).wait_recv()
            hop(j, hops - 1).wait_recv()
            total = dense[j % 5, layer] + zin[j, half - 1].astype(F32) + zin[j, hops - 1].astype(F32)
            cols = pl.ds(pl.multiple_of(j * wide, wide), wide)
            moe[:, cols] = (res_ref[:, cols].astype(F32) + total).astype(BF)

        for s in range(half - 1, 0, -1):
            @pl.when((i >= s) & (i < chunks + s))
            def _():
                stage(i - s, s)

        @pl.when(i < chunks)
        def _():
            for r in range(1, plane):
                pltpu.make_async_remote_copy(
                    src_ref=outgoing.at[i, spot],
                    dst_ref=incoming.at[i, spot],
                    send_sem=xs.at[i, r],
                    recv_sem=xr.at[i, r],
                    device_id=device(layer, spot + r),
                    device_id_type=MESH,
                ).wait_recv()
            rowsin = incoming[i].reshape(per_layer, wide)
            for z in range(layers):
                dense[i % 5, z] = mm(mixing[z * tokens : (z + 1) * tokens, :], rowsin)
            stage(i, 0)

        @pl.when(i == chunks)
        def _():
            for r in range(1, n_sa):
                copy_y(r).wait_recv()
            for q in range(1, n_sa):
                copy_last(q).start()

    stream = moe[...].astype(F32)
    scale = lax.rsqrt(jnp.mean(stream * stream, axis=-1, keepdims=True) + 1e-06)
    moe[...] = (stream * scale * gain_ref[...].astype(F32)).astype(BF)
    for q in range(n_sa):
        landed(q).wait_recv()

    pair = part // DV

    def pass_on(b):
        return pltpu.make_async_remote_copy(
            src_ref=later.at[b], dst_ref=earlier.at[b], send_sem=ss.at[b], recv_sem=sr.at[b],
            device_id={"sa": (y + 1) % n_sa}, device_id_type=MESH,
        )

    strips = weight.shape[0]

    @pl.loop(0, strips)
    def _(b):
        values = mm(moe[...], weight[b]).astype(BF)
        for h in range(pair):
            both = mm(mbo[b * pair + h], values[:, h * DV : (h + 1) * DV])
            both = both[: 2 * tokens] + both[2 * tokens :]
            fresh[b * pair + h] = both

        @pl.when(y == 0)
        def _():
            for h in range(pair):
                later[b, h] = fresh[b * pair + h, tokens:].astype(BF)
            pass_on(b).start()

    @pl.loop(0, strips)
    def _(b):
        cols = pl.ds(pl.multiple_of(b * part, part), part)

        @pl.when(y == 0)
        def _():
            parts = [fresh[b * pair + h, :tokens] for h in range(pair)]
            out_ref[:, cols] = jnp.concatenate(parts, axis=1).astype(BF)

        @pl.when(y > 0)
        def _():
            pass_on(b).wait_recv()

            @pl.when(y < n_sa - 1)
            def _():
                for h in range(pair):
                    at = b * pair + h
                    later[b, h] = (mm(amat[at], earlier[b, h]) + fresh[at, tokens:]).astype(BF)
                pass_on(b).start()

            parts = [
                fresh[b * pair + h, :tokens] + mm(gmat[b * pair + h], earlier[b, h]) for h in range(pair)
            ]
            out_ref[:, cols] = jnp.concatenate(parts, axis=1).astype(BF)

    @pl.when(y < n_sa - 1)
    def _():
        for b in range(strips):
            pass_on(b).wait_send()

    copy_beside().wait_send()
    for r in range(1, plane // 2):
        copy_x(r).wait_send()
    for r in range(1, layers):
        copy_z(r).wait_send()
    for r in range(1, n_sa):
        copy_y(r).wait_send()
    for q in range(n_sa):
        copy_last(q).wait_send()
    for r in range(1, layers):
        route_copy(r).wait_send()

    @pl.loop(0, chunks)
    def _(c):
        for r in range(1, plane):
            pltpu.make_async_remote_copy(
                src_ref=outgoing.at[c, spot],
                dst_ref=incoming.at[c, spot],
                send_sem=xs.at[c, r],
                recv_sem=xr.at[c, r],
                device_id=device(layer, spot + r),
                device_id_type=MESH,
            ).wait_send()
        for s in range(hops):
            hop(c, s).wait_send()


def layer(
    plane, expert_hidden, down_weight, residual, ids, amount, gain, value_weight, queries, keys, decay, rate
):
    exp_dev, rows, ff_units = expert_hidden.shape
    width = down_weight.shape[2]
    n_ea = lax.axis_size("ea")
    n_sa = lax.axis_size("sa")
    layers = n_ea // plane
    cap = rows // n_ea
    tokens, top = ids.shape
    wide = 256
    chunks = width // wide
    block = exp_dev * layers * cap
    source = np.arange(rows).reshape(layers, plane, cap).transpose(1, 0, 2).reshape(-1)
    order = np.zeros((rows, rows), np.float32)
    order[np.arange(rows), source] = 1.0
    strips = 2 * n_sa
    part = width // strips
    vmem = pl.BlockSpec(memory_space=pltpu.VMEM)
    hbm = pl.BlockSpec(memory_space=pl.ANY)
    dma = pltpu.SemaphoreType.DMA
    return pl.pallas_call(
        functools.partial(layer_kernel, plane, layers),
        out_shape=jax.ShapeDtypeStruct((tokens, width), BF),
        in_specs=[vmem, hbm] + [vmem] * 10,
        out_specs=vmem,
        scratch_shapes=[
            pltpu.VMEM((exp_dev, rows, ff_units), BF),
            pltpu.VMEM((3, exp_dev, ff_units, wide), BF),
            pltpu.VMEM((chunks, plane, block, wide), BF),
            pltpu.VMEM((chunks, plane, block, wide), BF),
            pltpu.VMEM((layers * tokens, plane * block), BF),
            pltpu.VMEM((5, layers, tokens, wide), F32),
            pltpu.VMEM((chunks, layers - 1, tokens, wide), BF),
            pltpu.VMEM((chunks, layers - 1, tokens, wide), BF),
            pltpu.VMEM((layers, 24, tokens), F32),
            pltpu.VMEM((tokens, width), BF),
            pltpu.VMEM((strips, width, part), BF),
            pltpu.VMEM((HV, 4 * tokens, tokens), BF),
            pltpu.VMEM((HV, DK, DK), BF),
            pltpu.VMEM((HV, tokens, DK), BF),
            pltpu.VMEM((4, tokens, 128), F32),
            pltpu.VMEM((HV, tokens + DK, DV), F32),
            pltpu.VMEM((strips, part // DV, DK, DV), BF),
            pltpu.VMEM((strips, part // DV, DK, DV), BF),
            dma((3,)),
            dma((chunks, plane)),
            dma((chunks, plane)),
            dma((chunks, layers - 1)),
            dma((chunks, layers - 1)),
            dma((layers,)),
            dma((layers,)),
            dma((18,)),
            dma((18,)),
            dma((strips,)),
            dma((strips,)),
        ],
        compiler_params=pltpu.CompilerParams(
            collective_id=0, has_side_effects=True, vmem_limit_bytes=63 * 1024 * 1024
        ),
        cost_estimate=pl.CostEstimate(flops=60_000_000_000, bytes_accessed=12_000_000, transcendentals=0),
        name="layer",
    )(
        expert_hidden, down_weight, jnp.asarray(order, BF), ids, amount, residual,
        gain.reshape(1, width), value_weight, queries, keys, decay, rate,
    )


def solution(mesh):
    def body(
        expert_hidden, down_weight, residual, expert_ids, combine_weight, norm_gain, value_weight,
        queries, keys, log_decay, write_rate,
    ):
        return layer(
            8, expert_hidden, down_weight, residual[0], expert_ids[0], combine_weight[0], norm_gain,
            value_weight, queries[0], keys[0], log_decay[0], write_rate[0],
        )[None]

    return jax.shard_map(
        body,
        mesh=mesh,
        in_specs=(
            P("ea", "sa", None),
            P("ea", None, None),
            P("ea", "sa", None),
            P("ea", "sa", None),
            P("ea", "sa", None),
            P(),
            P("ea", None),
            P("ea", "sa", None),
            P("ea", "sa", None),
            P("ea", "sa", None),
            P("ea", "sa", None),
        ),
        out_specs=P("ea", "sa", None),
        check_vma=False,
    )
```

time: 269 us -> 142 us (0.53)
  waiting for transfers between devices: 102 us -> 0 us
  between operations: 13.5 us -> 0.01 us
  starting transfers between devices: 6.67 us -> 0 us
  Pallas kernels: 137 us -> 133 us
    all_gather x2 -> x0, waiting for transfers between devices: 82 us -> none  [the longest x1 82 us: on_device(): strip = lax.all_gather(strip, 'ea', axis=0, tiled=True)]
    ppermute x5 -> x0, waiting for transfers between devices: 20.4 us -> none  [shifted(): return lax.ppermute(field, 'sa', [(i, i + by) for i in range(n_sa - by)])]
    ppermute x5 -> x0, starting transfers between devices: 6.62 us -> none  [shifted(): return lax.ppermute(field, 'sa', [(i, i + by) for i in range(n_sa - by)])]
    pallas_call x5 -> x1, Pallas kernels: 137 us -> 133 us  [layer(): pl.pallas_call(functools.partial(layer_kernel, plane, layers), out_shape=...]
    unnamed x26 -> x5, local copies, waits for them, and re-layouts: 4.45 us -> 7.54 us
  transfers between devices with their start and end apart: 7 -> 0, of which waited for: 2 -> 0; matrix products, arithmetic and copies ran while one was open for 1% -> 0% of each run, Pallas kernels for 50% -> 0%
where the time goes in v2:
time: 142 us
  Pallas kernels  133 us (94%)
  local copies, waits for them, and re-layouts  8.83 us (6%)
    pallas_call x1, Pallas kernels, layer(): pl.pallas_call(functools.partial(layer_kernel, plane, layers), out_shape=...  133 us
    unnamed x5, local copies, waits for them, and re-layouts  7.54 us

profile of v2, /device:TPU:24, one launch (start us, length us, event | category | flops | bytes accessed | tf_op | source)
XLA Modules:
  0.0 141.6 jit_solution(4435652330227077809)
XLA Ops:
  0.0 1.3 reshape.3.gain_ref
  1.3 1.4 %copy.13 = s32[1,128,10]{2,1,0:T(8,128)} copy(s32[1,128,10]{1,0,2:T(1,128)} %param.15) | data formatting | bytes 10240 | tf_op args[3]
  2.7 1.4 copy.14
  4.1 1.4 copy.15
  5.5 1.4 copy.16
  6.9 132.7 %layer.1 = bf16[128,2048]{1,0:T(8,128)(2,1)} custom-call(bf16[4,448,512]{2,1,0:T(8,128)(2,1)} %hid_ref.1, bf16[4,512,2048]{2,1,0:T(8,128)(2,1)} %down_ref.1, bf16[448,448]{1,0:T(8,128)(2,1)} %constant.2.clone.order_ref, s32[128,10]{1,0:T(8,128)} %bitcast.11, f32[128,10]{1,0:T(8,128)} %bitcast.12, bf16[128,2048]{1,0:T(8,128)(2,1)} %bitcast.13, ...), custom_call_target="tpu_custom_call" | custom-call | flops 60000002048 | bytes 12000000 | tf_op jit(solution)/shard_map/layer/pallas_call | solution.py:496
  139.7 1.9 %copy.18 = bf16[1,128,2048]{2,1,0:T(8,128)(2,1)} copy(bf16[1,128,2048]{2,1,0:T(8,128)(2,1)} %bitcast.8) | data formatting | bytes 1048576

commit v3 on v2

--- a/solution.py
+++ b/solution.py
@@ -58,17 +58,15 @@
 
 
 def gates(decay_ref, rate_ref, gate):
-    n, heads = decay_ref.shape
+    heads, n = decay_ref.shape
     row = lax.broadcasted_iota(jnp.int32, (n, n), 0)
     col = lax.broadcasted_iota(jnp.int32, (n, n), 1)
-    blank = jnp.zeros((n, n - heads), F32)
-    summed = mm_full(
-        jnp.where(row >= col, 1.0, 0.0), jnp.concatenate([decay_ref[...], blank], axis=1)
-    )
-    gate[0] = summed
-    gate[1] = jnp.transpose(summed)
-    gate[2] = jnp.concatenate([rate_ref[...], blank], axis=1)
-    gate[3] = jnp.transpose(jnp.concatenate([rate_ref[...], blank], axis=1))
+    blank = jnp.zeros((n - heads, n), F32)
+    summed = mm_full(decay_ref[...], jnp.where(row <= col, 1.0, 0.0))
+    for at, rows in ((0, summed), (2, rate_ref[...])):
+        rows = jnp.concatenate([rows, blank], axis=0)
+        gate[at] = jnp.transpose(rows)
+        gate[at + 1] = rows
 
 
 def prepare_heads(step, q_ref, k_ref, gate, mbo_ref, a_ref, g_ref):
@@ -127,8 +125,15 @@
     dsem, xs, xr, zs, zr, rs, rr, ws, wr, ss, sr,
 ):
     exp_dev, rows, _ = hid_ref.shape
-    tokens, top = ids_ref.shape
-    chunks, _, block, wide = outgoing.shape
+    top, _, tokens = ids_ref.shape
+    _, chunks, block, wide = outgoing.shape
+    full = chunks - 1
+    units = chunks + 1
+
+    def span(u):
+        if isinstance(u, int) and u >= full:
+            return full, (u - full) * (wide // 2), wide // 2
+        return u, 0, wide
     cap = rows // (plane * layers)
     group = layers * cap
     per_layer = plane * block
@@ -161,7 +166,6 @@
         pl.semaphore_signal(barrier, inc=1, device_id=device(layer + r, spot), device_id_type=MESH)
     for r in range(1, n_sa):
         pl.semaphore_signal(barrier, inc=1, device_id={"sa": (y + r) % n_sa}, device_id_type=MESH)
-    pl.semaphore_wait(barrier, plane + layers + n_sa - 3)
 
     own_rows, part = value_ref.shape[0], weight.shape[2]
 
@@ -199,32 +203,28 @@
         ref = weight.at[((y + q) % n_sa) * 2 + 1 - core]
         return remote(ref, ref, 14 + (y + q) % n_sa, {"ea": me + 1 - 2 * core})
 
-    copy_beside().start()
     weight[strip, pl.ds(pl.multiple_of(me * own_rows, own_rows), own_rows)] = value_ref[
         :, pl.ds(pl.multiple_of(strip * part, part), part)
     ]
 
     experts = exp_dev * plane * layers
-    lane = lax.broadcasted_iota(jnp.int32, (tokens, experts), 1)
-    ids = ids_ref[...]
-    counts = jnp.zeros((tokens, experts), F32)
+    name = lax.broadcasted_iota(jnp.int32, (experts, tokens), 0)
+    counts = jnp.zeros((experts, tokens), F32)
     for i in range(top):
-        counts += jnp.where(lane == ids[:, i : i + 1], 1.0, 0.0)
+        counts += jnp.where(name == ids_ref[i], 1.0, 0.0)
     trow = lax.broadcasted_iota(jnp.int32, (tokens, tokens), 0)
     tcol = lax.broadcasted_iota(jnp.int32, (tokens, tokens), 1)
-    prior = mm(jnp.where(trow > tcol, 1.0, 0.0), counts)
-    place = (ids // exp_dev) * block + (ids % exp_dev) * group
-    columns = []
+    prior = mm(counts, jnp.where(trow < tcol, 1.0, 0.0))
+    found = []
     for i in range(top):
-        slot = jnp.sum(jnp.where(lane == ids[:, i : i + 1], prior, 0.0), axis=1, keepdims=True)
-        columns.append(place[:, i : i + 1].astype(F32) + slot)
-    columns += [amount_ref[:, i : i + 1] for i in range(top)]
-    table = jnp.zeros((tokens, 128), F32)
-    tl = lax.broadcasted_iota(jnp.int32, (tokens, 128), 1)
-    for i, column in enumerate(columns):
-        table = jnp.where(tl == i, column, table)
+        ids = ids_ref[i]
+        slot = jnp.sum(jnp.where(name == ids, prior, 0.0), axis=0, keepdims=True)
+        place = (ids // exp_dev) * block + (ids % exp_dev) * group
+        found.append(place.astype(F32) + slot)
+    found += [amount_ref[i] for i in range(top)]
     deep = routes.shape[1]
-    routes[layer] = jnp.transpose(table)[:deep]
+    found.append(jnp.zeros((deep - 2 * top, tokens), F32))
+    routes[layer] = jnp.concatenate(found, axis=0)
 
     for e in range(exp_dev):
         hidden[e] = mm(order_ref[...], hid_ref[e]).astype(BF)
@@ -239,45 +239,67 @@
             device_id_type=MESH,
         )
 
-    for r in range(1, layers):
-        route_copy(r).start()
-
-    copy_beside().wait_recv()
-    for r in range(1, plane // 2):
-        copy_x(r).start()
-
     def produce(c):
         chunk_copy(c).wait()
         made = [mm(hidden[e], down[c % depth, e]) for e in range(exp_dev)]
         for p in range(plane):
             mine = [m[p * group : (p + 1) * group] for m in made]
-            outgoing[c, p] = jnp.concatenate(mine, axis=0).astype(BF)
+            outgoing[p, c] = jnp.concatenate(mine, axis=0).astype(BF)
 
         @pl.when(c + depth < chunks)
         def _():
             chunk_copy(c + depth).start()
 
-    def ship(c):
-        for r in range(1, plane):
-            to = (spot + r) % plane
+    def block_of(ref, p, u):
+        c, at, size = span(u)
+        return ref.at[p, c, :, pl.ds(at, size)]
+
+    def ship(u):
+        def send(to):
             pltpu.make_async_remote_copy(
-                src_ref=outgoing.at[c, to],
-                dst_ref=incoming.at[c, spot],
-                send_sem=xs.at[c, r],
-                recv_sem=xr.at[c, r],
+                src_ref=block_of(outgoing, to, u),
+                dst_ref=block_of(incoming, spot, u),
+                send_sem=xs.at[u],
+                recv_sem=xr.at[u],
                 device_id=device(layer, to),
                 device_id_type=MESH,
             ).start()
-        incoming[c, spot] = outgoing[c, spot]
+
+        for c in range(2):
+            for dx in (2, 1, 3):
+                send(((near + sign * dx + plane) % (plane // 2)) * 2 + c)
+        send(spot + 1 - 2 * core)
+        c, at, size = span(u)
+        incoming[spot, c, :, at : at + size] = outgoing[spot, c, :, at : at + size]
+
+    def shipped(u):
+        return pltpu.make_async_remote_copy(
+            src_ref=block_of(outgoing, pl.ds(0, plane - 1), u),
+            dst_ref=block_of(incoming, pl.ds(0, plane - 1), u),
+            send_sem=xs.at[u],
+            recv_sem=xr.at[u],
+            device_id=device(layer, spot + 1),
+            device_id_type=MESH,
+        )
 
     produce(0)
-
-    @pl.loop(1, chunks)
+    pl.semaphore_wait(barrier, plane + layers + n_sa - 3)
+    copy_beside().start()
+    for r in range(1, layers):
+        route_copy(r).start()
+    produce(1)
+    copy_beside().wait_recv()
+    for r in range(1, plane // 2):
+        copy_x(r).start()
+    ship(0)
+
+    @pl.loop(2, chunks)
     def _(c):
         produce(c)
         ship(c - 1)
 
-    ship(chunks - 1)
+    ship(full)
+    ship(full + 1)
 
     for r in range(1, plane // 2):
         copy_x(r).wait_recv()
@@ -315,11 +337,11 @@
 
     def hop(j, s):
         ahead = s < half
-        step = s if ahead else s - half
         way = sign if ahead else -sign
+        c, at, size = span(j)
         return pltpu.make_async_remote_copy(
-            src_ref=zout.at[j, s],
-            dst_ref=zin.at[j, s],
+            src_ref=zout.at[c, s, :, pl.ds(at, size)],
+            dst_ref=zin.at[c, s, :, pl.ds(at, size)],
             send_sem=zs.at[j, s],
             recv_sem=zr.at[j, s],
             device_id=device(layer + way, spot),
@@ -333,69 +355,128 @@
 
     hops = layers - 1
 
+    def came(j, h):
+        hop(j, h).wait_recv()
+        c, at, size = span(j)
+        return zin[c, h, :, at : at + size].astype(F32)
+
     def stage(j, s):
-        sent = []
-        for h in (s, s + half):
-            if (h < half) == (h == s) and h < hops:
-                part = dense[j % 5, target(h)]
-                if s > 0:
-                    hop(j, h - 1).wait_recv()
-                    part = part + zin[j, h - 1].astype(F32)
-                zout[j, h] = part.astype(BF)
-                sent.append(h)
+        c, at, size = span(j)
+        sent = [h for h in (s, s + half) if h < hops]
+        for h in sent:
+            part = dense[j % 5, target(h), :, :size]
+            if s > 0:
+                part = part + came(j, h - 1)
+            zout[c, h, :, at : at + size] = part.astype(BF)
         for h in sent:
             hop(j, h).start()
 
-    @pl.loop(0, chunks + half)
+    def last(j):
+        c, at, size = span(j)
+        total = dense[j % 5, layer, :, :size] + came(j, half - 1) + came(j, hops - 1)
+        start = c * wide + at
+        cols = pl.ds(start if isinstance(c, int) else pl.multiple_of(start, wide), size)
+        moe[:, cols] = (res_ref[:, cols].astype(F32) + total).astype(BF)
+
+    def mix_layer(j, z):
+        c, at, size = span(j)
+        start = pl.ds(pl.multiple_of(z * tokens, tokens), tokens)
+        rowsin = incoming[:, c, :, at : at + size].reshape(per_layer, size)
+        dense[j % 5, z, :, :size] = mm(mixing[start, :], rowsin)
+
+    def straight(j, k):
+        c, at, size = span(j)
+        return pltpu.make_async_remote_copy(
+            src_ref=zout.at[c, k - 1, :, pl.ds(at, size)],
+            dst_ref=zin.at[c, k - 1, :, pl.ds(at, size)],
+            send_sem=zs.at[j, k - 1],
+            recv_sem=zr.at[j, k - 1],
+            device_id=device(layer + k, spot),
+            device_id_type=MESH,
+        )
+
+    def arrive_last(j):
+        c, at, size = span(j)
+        shipped(j).wait_recv()
+        order = sorted(range(1, layers), key=lambda k: -min(k, layers - k))
+        waiting = []
+        for k in order:
+            mix_layer(j, (layer + k) % layers)
+            zout[c, k - 1, :, at : at + size] = dense[j % 5, (layer + k) % layers, :, :size].astype(BF)
+            if waiting:
+                straight(j, waiting.pop()).start()
+            waiting.append(k)
+        mix_layer(j, layer)
+        straight(j, waiting.pop()).start()
+
+    def finish_last(j):
+        c, at, size = span(j)
+        total = dense[j % 5, layer, :, :size]
+        for k in range(1, layers):
+            straight(j, k).wait_recv()
+            total = total + zin[c, k - 1, :, at : at + size].astype(F32)
+        cols = pl.ds(c * wide + at, size)
+        moe[:, cols] = (res_ref[:, cols].astype(F32) + total).astype(BF)
+
+    def arrive(j):
+        shipped(j).wait_recv()
+        mix_layer(j, target(0))
+        mix_layer(j, target(half))
+        stage(j, 0)
+        for k in range(layers):
+            if k not in (half, half + 1):
+                mix_layer(j, (layer + sign * k + 2 * layers) % layers)
+
+    @pl.loop(0, full)
     def _(i):
         @pl.when(i >= half)
         def _():
-            j = i - half
-            hop(j, half - 1).wait_recv()
-            hop(j, hops - 1).wait_recv()
-            total = dense[j % 5, layer] + zin[j, half - 1].astype(F32) + zin[j, hops - 1].astype(F32)
-            cols = pl.ds(pl.multiple_of(j * wide, wide), wide)
-            moe[:, cols] = (res_ref[:, cols].astype(F32) + total).astype(BF)
+            last(i - half)
 
         for s in range(half - 1, 0, -1):
-            @pl.when((i >= s) & (i < chunks + s))
+
+            @pl.when(i >= s)
             def _():
                 stage(i - s, s)
 
-        @pl.when(i < chunks)
-        def _():
-            for r in range(1, plane):
-                pltpu.make_async_remote_copy(
-                    src_ref=outgoing.at[i, spot],
-                    dst_ref=incoming.at[i, spot],
-                    send_sem=xs.at[i, r],
-                    recv_sem=xr.at[i, r],
-                    device_id=device(layer, spot + r),
-                    device_id_type=MESH,
-                ).wait_recv()
-            rowsin = incoming[i].reshape(per_layer, wide)
-            for z in range(layers):
-                dense[i % 5, z] = mm(mixing[z * tokens : (z + 1) * tokens, :], rowsin)
-            stage(i, 0)
-
-        @pl.when(i == chunks)
-        def _():
-            for r in range(1, n_sa):
+        arrive(i)
+
+    for i in range(full, full + 1 + half):
+        if i - half < full:
+            last(i - half)
+        for s in range(half - 1, 0, -1):
+            if i - s <= full:
+                stage(i - s, s)
+        if i == full:
+            arrive(i)
+        if i == full + 1:
+            arrive_last(i)
+        if i == full + 2:
+            for r in (1, n_sa - 1):
                 copy_y(r).wait_recv()
-            for q in range(1, n_sa):
-                copy_last(q).start()
+                copy_last(n_sa - r).start()
+        if i == full + half:
+            for r in range(2, n_sa - 1):
+                copy_y(r).wait_recv()
+                copy_last(n_sa - r).start()
+    last(full)
+    finish_last(full + 1)
 
     stream = moe[...].astype(F32)
     scale = lax.rsqrt(jnp.mean(stream * stream, axis=-1, keepdims=True) + 1e-06)
-    moe[...] = (stream * scale * gain_ref[...].astype(F32)).astype(BF)
+    stream = stream * scale
+    gain = gain_ref[...].astype(F32)
+    for g in range(gain.shape[0]):
+        cols = slice(g * 128, (g + 1) * 128)
+        moe[:, cols] = (stream[:, cols] * gain[g : g + 1]).astype(BF)
     for q in range(n_sa):
         landed(q).wait_recv()
 
     pair = part // DV
 
-    def pass_on(b):
+    def pass_on(at):
         return pltpu.make_async_remote_copy(
-            src_ref=later.at[b], dst_ref=earlier.at[b], send_sem=ss.at[b], recv_sem=sr.at[b],
+            src_ref=later.at[at], dst_ref=earlier.at[at], send_sem=ss.at[at], recv_sem=sr.at[at],
             device_id={"sa": (y + 1) % n_sa}, device_id_type=MESH,
         )
 
@@ -412,8 +493,9 @@
         @pl.when(y == 0)
         def _():
             for h in range(pair):
-                later[b, h] = fresh[b * pair + h, tokens:].astype(BF)
-            pass_on(b).start()
+                later[b * pair + h] = fresh[b * pair + h, tokens:].astype(BF)
+            for h in range(pair):
+                pass_on(b * pair + h).start()
 
     @pl.loop(0, strips)
     def _(b):
@@ -426,24 +508,24 @@
 
         @pl.when(y > 0)
         def _():
-            pass_on(b).wait_recv()
-
-            @pl.when(y < n_sa - 1)
-            def _():
-                for h in range(pair):
-                    at = b * pair + h
-                    later[b, h] = (mm(amat[at], earlier[b, h]) + fresh[at, tokens:]).astype(BF)
-                pass_on(b).start()
+            for h in range(pair):
+                at = b * pair + h
+                pass_on(at).wait_recv()
+
+                @pl.when(y < n_sa - 1)
+                def _():
+                    later[at] = (mm(amat[at], earlier[at]) + fresh[at, tokens:]).astype(BF)
+                    pass_on(at).start()
 
             parts = [
-                fresh[b * pair + h, :tokens] + mm(gmat[b * pair + h], earlier[b, h]) for h in range(pair)
+                fresh[b * pair + h, :tokens] + mm(gmat[b * pair + h], earlier[b * pair + h]) for h in range(pair)
             ]
             out_ref[:, cols] = jnp.concatenate(parts, axis=1).astype(BF)
 
     @pl.when(y < n_sa - 1)
     def _():
-        for b in range(strips):
-            pass_on(b).wait_send()
+        for at in range(strips * pair):
+            pass_on(at).wait_send()
 
     copy_beside().wait_send()
     for r in range(1, plane // 2):
@@ -457,19 +539,19 @@
     for r in range(1, layers):
         route_copy(r).wait_send()
 
-    @pl.loop(0, chunks)
-    def _(c):
-        for r in range(1, plane):
-            pltpu.make_async_remote_copy(
-                src_ref=outgoing.at[c, spot],
-                dst_ref=incoming.at[c, spot],
-                send_sem=xs.at[c, r],
-                recv_sem=xr.at[c, r],
-                device_id=device(layer, spot + r),
-                device_id_type=MESH,
-            ).wait_send()
+    def drained(u):
+        shipped(u).wait_send()
         for s in range(hops):
-            hop(c, s).wait_send()
+            hop(u, s).wait_send()
+
+    @pl.loop(0, full)
+    def _(u):
+        drained(u)
+
+    drained(full)
+    shipped(full + 1).wait_send()
+    for k in range(1, layers):
+        straight(full + 1, k).wait_send()
 
 
 def layer(
@@ -481,7 +563,7 @@
     n_sa = lax.axis_size("sa")
     layers = n_ea // plane
     cap = rows // n_ea
-    tokens, top = ids.shape
+    top, _, tokens = ids.shape
     wide = 256
     chunks = width // wide
     block = exp_dev * layers * cap
@@ -501,8 +583,8 @@
         scratch_shapes=[
             pltpu.VMEM((exp_dev, rows, ff_units), BF),
             pltpu.VMEM((3, exp_dev, ff_units, wide), BF),
-            pltpu.VMEM((chunks, plane, block, wide), BF),
-            pltpu.VMEM((chunks, plane, block, wide), BF),
+            pltpu.VMEM((plane, chunks, block, wide), BF),
+            pltpu.VMEM((plane, chunks, block, wide), BF),
             pltpu.VMEM((layers * tokens, plane * block), BF),
             pltpu.VMEM((5, layers, tokens, wide), F32),
             pltpu.VMEM((chunks, layers - 1, tokens, wide), BF),
@@ -515,19 +597,19 @@
             pltpu.VMEM((HV, tokens, DK), BF),
             pltpu.VMEM((4, tokens, 128), F32),
             pltpu.VMEM((HV, tokens + DK, DV), F32),
-            pltpu.VMEM((strips, part // DV, DK, DV), BF),
-            pltpu.VMEM((strips, part // DV, DK, DV), BF),
+            pltpu.VMEM((HV, DK, DV), BF),
+            pltpu.VMEM((HV, DK, DV), BF),
             dma((3,)),
-            dma((chunks, plane)),
-            dma((chunks, plane)),
-            dma((chunks, layers - 1)),
-            dma((chunks, layers - 1)),
+            dma((chunks + 1,)),
+            dma((chunks + 1,)),
+            dma((chunks + 1, layers - 1)),
+            dma((chunks + 1, layers - 1)),
             dma((layers,)),
             dma((layers,)),
             dma((18,)),
             dma((18,)),
-            dma((strips,)),
-            dma((strips,)),
+            dma((HV,)),
+            dma((HV,)),
         ],
         compiler_params=pltpu.CompilerParams(
             collective_id=0, has_side_effects=True, vmem_limit_bytes=63 * 1024 * 1024
@@ -536,7 +618,7 @@
         name="layer",
     )(
         expert_hidden, down_weight, jnp.asarray(order, BF), ids, amount, residual,
-        gain.reshape(1, width), value_weight, queries, keys, decay, rate,
+        gain.reshape(width // 128, 128), value_weight, queries, keys, decay, rate,
     )
 
 
@@ -546,8 +628,9 @@
         queries, keys, log_decay, write_rate,
     ):
         return layer(
-            8, expert_hidden, down_weight, residual[0], expert_ids[0], combine_weight[0], norm_gain,
-            value_weight, queries[0], keys[0], log_decay[0], write_rate[0],
+            8, expert_hidden, down_weight, residual[0], expert_ids.transpose(2, 0, 1),
+            combine_weight.transpose(2, 0, 1), norm_gain, value_weight, queries[0], keys[0],
+            log_decay[0].T, write_rate[0].T,
         )[None]
 
     return jax.shard_map(

time: 142 us -> 131 us (0.923)
  local copies, waits for them, and re-layouts: 8.83 us -> 1.88 us
  Pallas kernels: 133 us -> 129 us
    unnamed x5 -> x1, local copies, waits for them, and re-layouts: 7.54 us -> 1.88 us
    pallas_call x1, Pallas kernels: 133 us -> 129 us  [layer(): pl.pallas_call(functools.partial(layer_kernel, plane, layers), out_shape=...]
where the time goes in v3:
time: 131 us; the launch traced here: 130 us
  Pallas kernels  129 us (98%)
  local copies, waits for them, and re-layouts  1.88 us (1%)
    pallas_call x1, Pallas kernels, layer(): pl.pallas_call(functools.partial(layer_kernel, plane, layers), out_shape=...  129 us

profile of v3, /device:TPU:24, one launch (start us, length us, event | category | flops | bytes accessed | tf_op | source)
XLA Modules:
  0.0 130.4 jit_solution(5998886938539348079)
XLA Ops:
  0.0 128.5 %layer.1 = bf16[128,2048]{1,0:T(8,128)(2,1)} custom-call(bf16[4,448,512]{2,1,0:T(8,128)(2,1)} %hid_ref.1, bf16[4,512,2048]{2,1,0:T(8,128)(2,1)} %down_ref.1, bf16[448,448]{1,0:T(8,128)(2,1)} %constant.2.clone.order_ref, s32[10,1,128]{2,1,0:T(1,128)} %bitcast.19, f32[10,1,128]{2,1,0:T(1,128)} %bitcast.20, bf16[128,2048]{1,0:T(8,128)(2,1)} %bitcast.14, ...), custom_call_target="tpu_custom_call" | custom-call | flops 60000002048 | bytes 12000000 | tf_op jit(solution)/shard_map/layer/pallas_call | solution.py:578
  128.5 1.9 %copy.14 = bf16[1,128,2048]{2,1,0:T(8,128)(2,1)} copy(bf16[1,128,2048]{2,1,0:T(8,128)(2,1)} %bitcast.13) | data formatting | bytes 1048576

commit v4 on v3

--- a/solution.py
+++ b/solution.py
@@ -293,18 +293,24 @@
         copy_x(r).start()
     ship(0)
 
-    @pl.loop(2, chunks)
+    @pl.loop(2, chunks // 2 + 1)
     def _(c):
         produce(c)
         ship(c - 1)
-
-    ship(full)
-    ship(full + 1)
 
     for r in range(1, plane // 2):
         copy_x(r).wait_recv()
     for r in range(1, layers):
         copy_z(r).start()
+
+    @pl.loop(chunks // 2 + 1, chunks)
+    def _(c):
+        produce(c)
+        ship(c - 1)
+
+    ship(full)
+    ship(full + 1)
+
     for r in range(1, layers):
         route_copy(r).wait_recv()
 

time: 131 us -> 131 us (level)
  no operation moved by 1% of the time
where the time goes in v4:
time: 131 us; the launch traced here: 130 us
  Pallas kernels  129 us (98%)
  local copies, waits for them, and re-layouts  1.88 us (1%)
    pallas_call x1, Pallas kernels, layer(): pl.pallas_call(functools.partial(layer_kernel, plane, layers), out_shape=...  129 us

profile of v4, /device:TPU:24, one launch (start us, length us, event | category | flops | bytes accessed | tf_op | source)
XLA Modules:
  0.0 130.4 jit_solution(2011429724278593304)
XLA Ops:
  0.0 128.5 %layer.1 = bf16[128,2048]{1,0:T(8,128)(2,1)} custom-call(bf16[4,448,512]{2,1,0:T(8,128)(2,1)} %hid_ref.1, bf16[4,512,2048]{2,1,0:T(8,128)(2,1)} %down_ref.1, bf16[448,448]{1,0:T(8,128)(2,1)} %constant.2.clone.order_ref, s32[10,1,128]{2,1,0:T(1,128)} %bitcast.19, f32[10,1,128]{2,1,0:T(1,128)} %bitcast.20, bf16[128,2048]{1,0:T(8,128)(2,1)} %bitcast.14, ...), custom_call_target="tpu_custom_call" | custom-call | flops 60000002048 | bytes 12000000 | tf_op jit(solution)/shard_map/layer/pallas_call | solution.py:584
  128.5 1.9 %copy.14 = bf16[1,128,2048]{2,1,0:T(8,128)(2,1)} copy(bf16[1,128,2048]{2,1,0:T(8,128)(2,1)} %bitcast.13) | data formatting | bytes 1048576
